TPU v7x, 32 devices: a whole 2x2x4 slice. The times are simulated.
32 devices in a mesh: batch: 4 (over y, x), field: 2 (over core), dim: 4 (over z).
Axes of the slice: x: 2, y: 2, z: 4, core: 2. Of those that a mesh axis runs over, the one named last changes fastest.
Arguments:
- features: bfloat16 [26, 128, 4096], P('field', 'dim', 'batch'), may hold values from -6 to 6
- cross_weight: bfloat16 [2, 26, 128, 26, 128], P(None, 'field', 'dim'), may hold values from -0.109375 to 0.109375
- cross_bias: float32 [2, 26, 128], P(None, 'field', 'dim'), may hold values from -3 to 3
- tower_weight: bfloat16 [1024, 26, 128], P(('field', 'dim')), may hold values from -0.109375 to 0.109375
- tower_bias: float32 [1024], P(('field', 'dim')), may hold values from -3 to 3
- query_weight: bfloat16 [1024, 128], P(('field', 'dim')), may hold values from -0.1875 to 0.1875
- user_vec: bfloat16 [4096, 128], P('batch'), may hold values from -6 to 6
- candidates: bfloat16 [1024, 128], P('batch'), may hold values from -6 to 6
- positive: int32 [4096], P('batch'), may hold values from 0 to 1023
Outputs:
- crossed: bfloat16 [26, 128, 4096], P('field', 'dim', 'batch')
- losses: float32 [4096], P('batch')
All inputs are finite; a program needn't handle non-finite values.
Results may differ from a plain program's by a relative error of at most 0.0049.
Values may be sent and summed in bfloat16 or wider, within the bound.
A program may use at most 64 MiB of HBM per device.

v0:
```python
import functools
import math

import jax
import jax.numpy as jnp
from jax import lax
from jax.experimental import pallas as pl
from jax.experimental.pallas import tpu as pltpu
from jax.sharding import PartitionSpec as P

CROSS = 2
MESH = pl.DeviceIdType.MESH


def tower_levels(dim_count):
    held = min(2, dim_count)
    return (dim_count - held) // 2, held


def chunk_count(row_count, field_count, held):
    chunks = 2
    while chunks > field_count and row_count % (chunks * held * 128):
        chunks //= 2
    return chunks


def rank_kernel(
    counts, splits,
    feat, weight, bias, tower, tower_bias, query_weight, user, cand, positive,
    out, loss_out,
    x0, x1, flat, sent, rows, towers, biases, columns_bias, queries, cands, losses,
    feat_sem, weight_sem, tower_sem, small_sem,
    right_sem, left_sem, pair_sem, recv_sem, pair_recv,
    row_send, row_recv, chain_right, chain_left, chain_recv, both_send, both_recv,
    plane_send, plane_recv, plane_pair, plane_pair_recv,
    cand_send, cand_recv, loss_send, loss_recv,
):
    batch_count, field_count, dim_count = counts
    chunks, split = splits
    b = lax.axis_index("batch")
    f = lax.axis_index("field")
    d = lax.axis_index("dim")
    me = f * dim_count + d
    members = field_count * dim_count
    fl, el, row_count = feat.shape
    columns = fl * el
    fields, width, rc = x0.shape[1:]
    low, held = tower_levels(dim_count)
    high = low + held - 1
    level_of = d - low
    active = (d >= low) & (d <= high)
    sub = rc // held
    run = chunks // field_count
    share = run * sub
    part = towers.shape[2]
    units = split * part
    buffers = (x0, x1)
    other = field_count - 1 - f
    mine = b if split > 1 else 0
    to_right = jnp.minimum(d + 1, dim_count - 1)
    to_left = jnp.maximum(d - 1, 0)

    def remote(ref, send, recv, **where):
        return pltpu.make_async_remote_copy(
            ref, ref, send, recv, device_id=where, device_id_type=MESH)

    def place(ff, o):
        return pl.ds(ff * fl, fl), pl.ds(pl.multiple_of(o * el, el), el)

    def piece(ph, c, ff, o):
        fs, ds = place(ff, o)
        return buffers[ph].at[c, fs, ds, :]

    def right(ph, c, o):
        return remote(piece(ph, c, f, o), right_sem.at[ph, c, o], recv_sem.at[ph, c, o], dim=to_right)

    def left(ph, c, o):
        return remote(piece(ph, c, f, o), left_sem.at[ph, c, o], recv_sem.at[ph, c, o], dim=to_left)

    def pair(ph, c, o, ff):
        return remote(
            piece(ph, c, ff, o), pair_sem.at[ph, c, o], pair_recv.at[ph, c, o], field=other)

    def issue_own(ph, c):
        @pl.when(d < dim_count - 1)
        def _():
            right(ph, c, d).start()

        @pl.when(d > 0)
        def _():
            left(ph, c, d).start()

        pair(ph, c, d, f).start()

    def forwards(ph, c):
        for s in range(1, dim_count):
            @pl.when(d - s >= 0)
            def _():
                right(ph, c, d - s).wait_recv()

                @pl.when(d < dim_count - 1)
                def _():
                    right(ph, c, d - s).start()

                pair(ph, c, d - s, f).start()

            @pl.when(d + s < dim_count)
            def _():
                left(ph, c, d + s).wait_recv()

                @pl.when(d > 0)
                def _():
                    left(ph, c, d + s).start()

                pair(ph, c, d + s, f).start()
        for o in range(dim_count):
            pair(ph, c, o, other).wait_recv()

    def weight_copy(level, ff):
        return pltpu.make_async_copy(
            weight.at[level, :, ff],
            flat.at[level, :, :, pl.ds(pl.multiple_of(ff * width, width), width)],
            weight_sem.at[level, ff])

    def tower_copy(ff):
        return pltpu.make_async_copy(
            tower.at[ff, pl.ds(pl.multiple_of(mine * part, part), part), :],
            towers.at[mine, me, :, pl.ds(pl.multiple_of(ff * width, width), width)],
            tower_sem.at[ff])

    def each_field(act):
        def step(ff, carry):
            act(ff)
            return carry

        lax.fori_loop(0, fields, step, 0)

    small_refs = (
        lambda o: towers.at[mine, f * dim_count + o],
        lambda o: queries.at[:, f * dim_count + o],
        lambda o: biases.at[f * dim_count + o],
    )
    small_wide = (
        lambda ff: towers.at[mine, pl.ds(ff * dim_count, dim_count)],
        lambda ff: queries.at[:, pl.ds(ff * dim_count, dim_count)],
        lambda ff: biases.at[pl.ds(ff * dim_count, dim_count)],
    )

    def chain_to(k, o, sems, target):
        return remote(small_refs[k](o), sems.at[k, o], chain_recv.at[k, o], dim=target)

    def chain_own():
        for k in range(3):
            @pl.when(d < high)
            def _():
                chain_to(k, d, chain_right, to_right).start()

            @pl.when(d > low)
            def _():
                chain_to(k, d, chain_left, to_left).start()

    def chain_step(s):
        for k in range(3):
            @pl.when((d - s >= 0) & (d <= high))
            def _():
                chain_to(k, d - s, chain_right, to_right).wait_recv()

                @pl.when(d < high)
                def _():
                    chain_to(k, d - s, chain_right, to_right).start()

            @pl.when((d + s < dim_count) & (d >= low))
            def _():
                chain_to(k, d + s, chain_left, to_left).wait_recv()

                @pl.when(d > low)
                def _():
                    chain_to(k, d + s, chain_left, to_left).start()

    def both(k, ff):
        return remote(small_wide[k](ff), both_send.at[k], both_recv.at[k], field=other)

    def plane(t, source):
        return remote(
            towers.at[source, pl.ds(f * dim_count, dim_count)],
            plane_send.at[t], plane_recv.at[source], batch=t)

    def plane_both(source, ff):
        return remote(
            towers.at[source, pl.ds(ff * dim_count, dim_count)],
            plane_pair.at[source], plane_pair_recv.at[source], field=other)

    def cand_copy(t, source):
        return remote(cands.at[source], cand_send.at[t], cand_recv.at[source], batch=t)

    def loss_copy(m, ff, level):
        ref = losses.at[level, pl.ds(ff * run, run)]
        return remote(
            ref, loss_send.at[m], loss_recv.at[ff, level], field=m // dim_count, dim=m % dim_count)

    def row_copy(c, level):
        fs, ds = place(f, d)
        return pltpu.make_async_remote_copy(
            sent.at[c, level],
            rows.at[fs, ds, pl.ds(pl.multiple_of(lax.rem(c, run) * sub, sub), sub)],
            row_send.at[c, level], row_recv.at[lax.rem(c, run), me],
            device_id={"field": c // run, "dim": low + level}, device_id_type=MESH)

    def own_rows(c, level):
        return (c // run == f) & (level_of == level)

    def advance(ph, c):
        whole = buffers[ph][c].reshape(fields * width, rc)
        matrix = flat[ph].reshape(columns, fields * width)
        product = jnp.dot(matrix, whole, preferred_element_type=jnp.float32) + bias[ph]
        fs, ds = place(f, d)
        anchor = x0[c, fs, ds, :].astype(jnp.float32).reshape(columns, rc)
        current = buffers[ph][c, fs, ds, :].astype(jnp.float32).reshape(columns, rc)
        return (anchor * product + current).astype(jnp.bfloat16).reshape(fl, el, rc)

    own_copies = []
    for c in range(chunks):
        own_copies.append(pltpu.make_async_copy(
            feat.at[:, :, pl.ds(c * rc, rc)], piece(0, c, f, d), feat_sem.at[c]))
    small_copies = [
        pltpu.make_async_copy(query_weight, queries.at[:, me], small_sem.at[0]),
        pltpu.make_async_copy(tower_bias, biases.at[me], small_sem.at[1]),
        pltpu.make_async_copy(cand, cands.at[b], small_sem.at[2]),
    ]
    for copy in own_copies + small_copies:
        copy.start()
    each_field(lambda ff: tower_copy(ff).start())
    for level in range(CROSS):
        each_field(lambda ff: weight_copy(level, ff).start())

    barrier = pltpu.get_barrier_semaphore()
    for k in range(1, members):
        m = lax.rem(me + k, members)
        pl.semaphore_signal(
            barrier, inc=1, device_id={"field": m // dim_count, "dim": m % dim_count},
            device_id_type=MESH)
    for k in range(1, batch_count):
        pl.semaphore_signal(
            barrier, inc=1, device_id={"batch": lax.rem(b + k, batch_count)}, device_id_type=MESH)
    pl.semaphore_wait(barrier, members + batch_count - 2)
    for copy in own_copies:
        copy.wait()
    issue_own(0, 0)
    if chunks > 1:
        issue_own(0, 1)
    each_field(lambda ff: tower_copy(ff).wait())
    for copy in small_copies:
        copy.wait()
    chain_own()

    @pl.when(active)
    def _():
        for k in range(1, batch_count):
            cand_copy(lax.rem(b + k, batch_count), b).start()

    for level in range(CROSS):
        each_field(lambda ff: weight_copy(level, ff).wait())

    def first(c, carry):
        @pl.when(c + 2 < chunks)
        def _():
            issue_own(0, c + 2)

        forwards(0, c)
        fs, ds = place(f, d)
        x1[c, fs, ds, :] = advance(0, c)
        issue_own(1, c)

        for s in range(1, min(chunks, dim_count)):
            @pl.when(c == s)
            def _():
                chain_step(s)

        return carry

    lax.fori_loop(0, chunks, first, 0)
    for s in range(min(chunks, dim_count), dim_count):
        chain_step(s)

    @pl.when(active)
    def _():
        for k in range(3):
            both(k, f).start()
        if split > 1:
            for k in range(1, split):
                plane(lax.rem(b + k, split), b).start()

    def second(c, carry):
        forwards(1, c)
        new = advance(1, c)
        out[:, :, pl.ds(pl.multiple_of(c * rc, 128), rc)] = new
        for level in range(held):
            block = new[:, :, level * sub:(level + 1) * sub]

            @pl.when(own_rows(c, level))
            def _():
                fs, ds = place(f, d)
                rows[fs, ds, pl.ds(pl.multiple_of(lax.rem(c, run) * sub, sub), sub)] = block

            @pl.when(jnp.logical_not(own_rows(c, level)))
            def _():
                sent[c, level] = block
                row_copy(c, level).start()

        return carry

    lax.fori_loop(0, chunks, second, 0)

    def tower_block(s, query):
        matrix = towers[s].reshape(members * part, fields * width)
        pre = jnp.dot(
            matrix, rows[...].reshape(fields * width, share), preferred_element_type=jnp.float32)
        pre = pre + columns_bias[s].reshape(members * part, share)
        hidden = jnp.maximum(pre, 0.0).astype(jnp.bfloat16)
        return query + lax.dot_general(
            hidden, queries[s].reshape(members * part, width), (((0,), (0,)), ((), ())),
            preferred_element_type=jnp.float32)

    @pl.when(active)
    def _():
        if split > 1:
            for k in range(1, split):
                source = lax.rem(b + k, split)
                plane(source, source).wait_recv()
                plane_both(source, f).start()
        for k in range(3):
            both(k, other).wait_recv()
        for k in range(1, batch_count):
            source = lax.rem(b + k, batch_count)
            cand_copy(source, source).wait_recv()
        for m in range(members):
            block = jnp.broadcast_to(biases[m], (share, units)).T
            columns_bias[:, m] = block.reshape(split, part, share)
        if split > 1:
            for k in range(1, split):
                plane_both(lax.rem(b + k, split), other).wait_recv()
        for j in range(run):
            for k in range(1, members):
                m = lax.rem(me + k, members)
                fs, ds = place(m // dim_count, m % dim_count)
                remote(rows.at[fs, ds, pl.ds(j * sub, sub)], row_send.at[0, 0], row_recv.at[j, m],
                       field=m // dim_count, dim=m % dim_count).wait_recv()

        query = lax.fori_loop(0, split, tower_block, jnp.zeros((share, width), jnp.float32))
        all_cands = cands[...].reshape(-1, width)
        for j in range(run):
            c = f * run + j
            start = pl.multiple_of(c * rc + level_of * sub, sub)
            query_vec = (
                query[j * sub:(j + 1) * sub] + user[pl.ds(start, sub), :].astype(jnp.float32)
            ).astype(jnp.bfloat16)
            logits = lax.dot_general(
                all_cands, query_vec, (((1,), (1,)), ((), ())), preferred_element_type=jnp.float32
            ) * (1.0 / math.sqrt(width))
            labels = lax.broadcasted_iota(jnp.int32, logits.shape, 0)
            target = positive[c * held + level_of]
            picked = jnp.sum(jnp.where(labels == target, logits, 0.0), axis=0, keepdims=True)
            best = jnp.max(logits, axis=0, keepdims=True)
            total = jnp.sum(jnp.exp(logits - best), axis=0, keepdims=True)
            losses[level_of, c] = best + jnp.log(total) - picked
        for k in range(1, members):
            loss_copy(lax.rem(me + k, members), f, level_of).start()

    def drain(c, carry):
        for ph in range(CROSS):
            for o in range(dim_count):
                @pl.when((o <= d) & (d < dim_count - 1))
                def _():
                    right(ph, c, o).wait_send()

                @pl.when((o >= d) & (d > 0))
                def _():
                    left(ph, c, o).wait_send()

                pair(ph, c, o, f).wait_send()
        return carry

    lax.fori_loop(0, chunks, drain, 0)
    for k in range(3):
        for o in range(dim_count):
            @pl.when((o <= d) & (d < high))
            def _():
                chain_to(k, o, chain_right, to_right).wait_send()

            @pl.when((o >= d) & (d > low))
            def _():
                chain_to(k, o, chain_left, to_left).wait_send()

    @pl.when(active)
    def _():
        for k in range(3):
            both(k, f).wait_send()
        if split > 1:
            for k in range(1, split):
                t = lax.rem(b + k, split)
                plane(t, b).wait_send()
                plane_both(t, f).wait_send()
        for k in range(1, batch_count):
            cand_copy(lax.rem(b + k, batch_count), b).wait_send()
        for k in range(1, members):
            loss_copy(lax.rem(me + k, members), f, level_of).wait_send()

    for c in range(chunks):
        for level in range(held):
            @pl.when(jnp.logical_not(own_rows(c, level)))
            def _():
                row_copy(c, level).wait_send()

    for ff in range(field_count):
        for level in range(held):
            @pl.when(jnp.logical_not((f == ff) & (level_of == level)))
            def _():
                loss_copy(ff * dim_count + low + level, ff, level).wait_recv()

    for c in range(chunks):
        for level in range(held):
            loss_out[c * held + level] = losses[level, c]


def body(
    features, cross_weight, cross_bias, tower_weight, tower_bias, query_weight,
    user_vec, candidates, positive,
):
    counts = tuple(lax.axis_size(name) for name in ("batch", "field", "dim"))
    batch_count, field_count, dim_count = counts
    members = field_count * dim_count
    fl, el, row_count = features.shape
    columns = fl * el
    units, fields, width = tower_weight.shape
    low, held = tower_levels(dim_count)
    chunks = chunk_count(row_count, field_count, held)
    split = batch_count if units % (batch_count * 16) == 0 else 1
    part = units // split
    rc = row_count // chunks
    sub = rc // held
    run = chunks // field_count
    share = run * sub
    steps = (CROSS, chunks, dim_count)
    small = (3, dim_count)
    dma = pltpu.SemaphoreType.DMA
    vmem = pltpu.VMEM
    bf16 = jnp.bfloat16
    far = pl.BlockSpec(memory_space=pl.ANY)
    near = pl.BlockSpec(memory_space=pltpu.VMEM)
    crossed, losses = pl.pallas_call(
        functools.partial(rank_kernel, counts, (chunks, split)),
        out_shape=(
            jax.ShapeDtypeStruct(features.shape, bf16),
            jax.ShapeDtypeStruct((chunks * held, 1, sub), jnp.float32),
        ),
        in_specs=[far, far, near, far, far, far, near, far, near],
        out_specs=(near, near),
        scratch_shapes=[
            vmem((chunks, fields, width, rc), bf16),
            vmem((chunks, fields, width, rc), bf16),
            vmem((CROSS, fl, el, fields * width), bf16),
            vmem((chunks, held, fl, el, sub), bf16),
            vmem((fields, width, share), bf16),
            vmem((split, members, part, fields * width), bf16),
            vmem((members, 1, units), jnp.float32),
            vmem((split, members, part, share), jnp.float32),
            vmem((split, members, part, width), bf16),
            vmem((batch_count,) + candidates.shape, bf16),
            vmem((held, chunks, 1, sub), jnp.float32),
            dma((chunks,)), dma((CROSS, fields)), dma((fields,)), dma((3,)),
            dma(steps), dma(steps), dma(steps), dma(steps), dma(steps),
            dma((chunks, held)), dma((run, members)), dma(small), dma(small), dma(small),
            dma((3,)), dma((3,)),
            dma((split,)), dma((split,)), dma((split,)), dma((split,)),
            dma((batch_count,)), dma((batch_count,)), dma((members,)), dma((field_count, held)),
        ],
        compiler_params=pltpu.CompilerParams(
            collective_id=0, has_side_effects=True, vmem_limit_bytes=56 * 2**20),
        name="rank_forward",
    )(
        features,
        cross_weight.transpose(0, 1, 3, 2, 4),
        cross_bias.reshape(CROSS, columns, 1),
        tower_weight.transpose(1, 0, 2),
        tower_bias.reshape(1, units),
        query_weight.reshape(split, part, width),
        user_vec,
        candidates,
        positive.reshape(chunks * held, 1, sub),
    )
    return (crossed, losses.reshape(row_count))


def solution(mesh):
    placed = (
        P("field", "dim", "batch"),
        P(None, "field", "dim", None, None),
        P(None, "field", "dim"),
        P(("field", "dim"), None, None),
        P(("field", "dim")),
        P(("field", "dim"), None),
        P("batch", None),
        P("batch", None),
        P("batch"),
    )
    return jax.shard_map(
        body,
        mesh=mesh,
        in_specs=placed,
        out_specs=(P("field", "dim", "batch"), P("batch")),
        check_vma=False,
    )
```

profile of v0, /device:TPU:0, one launch (start us, length us, event | category | flops | bytes accessed | tf_op | source)
XLA Modules:
  0.0 153.5 jit_solution(7235508768854950380)
XLA Ops:
  0.6 0.7 copy.12
  1.3 1.2 reshape.24.bias
  2.5 147.6 %rank_forward.1 = (bf16[13,32,1024]{2,1,0:T(8,128)(2,1)}, f32[4,1,256]{2,1,0:T(1,128)}) custom-call(bf16[13,32,1024]{2,1,0:T(8,128)(2,1)} %feat.1, bf16[2,13,26,32,128]{4,3,2,1,0:T(8,128)(2,1)} %bitcast.6, f32[2,416,1]{2,1,0:T(8,128)} %reshape.24.bias, bf16[26,128,128]{2,1,0:T(8,128)(2,1)} %bitcast.7, f32[1,128]{1,0:T(1,128)} %bitcast.11, ...), custom_call_target="tpu_custom_call" | custom-call | tf_op jit(solution)/shard_map/rank_forward/pallas_call | solution.py:450
  150.1 2.1 %copy.16 = bf16[13,32,1024]{2,1,0:T(8,128)(2,1)} copy(bf16[13,32,1024]{2,1,0:T(8,128)(2,1)} %get-tuple-element.8) | data formatting | bytes 1703936
  152.3 1.3 copy.17
where the time goes:
time: 154 us
  Pallas kernels  148 us (96%)
  local copies, waits for them, and re-layouts  5.3 us (3%)
    pallas_call x1, Pallas kernels, body(): pl.pallas_call(functools.partial(rank_kernel, counts, (chunks, split)), o...  148 us
    unnamed x3, local copies, waits for them, and re-layouts  4.1 us

commit v1 on v0

--- a/solution.py
+++ b/solution.py
@@ -422,11 +422,635 @@
             loss_out[c * held + level] = losses[level, c]
 
 
+def line_pieces(count, parts):
+    base, extra = divmod(count, parts)
+    bounds, start = [], 0
+    for k in range(parts):
+        size = base + (k < extra)
+        bounds.append((start, size))
+        start += size
+    return bounds
+
+
+def line_fits(counts, features, tower_weight, candidates):
+    batch_count, field_count, dim_count = counts
+    fl, el, row_count = features.shape
+    units, fields, width = tower_weight.shape
+    return (
+        dim_count == 4 and batch_count == 4 and field_count == 2
+        and fields % 2 == 0 and fl >= PIECES and el % 32 == 0 and 4 * el == width and width == 128
+        and row_count % (CHUNKS * field_count * 128) == 0 and units % (16 * batch_count) == 0)
+
+
+PIECES = 4
+CHUNKS = 4
+
+
+def line_kernel(
+    counts,
+    feat, weight, bias, tower, tower_bias, query_weight, user, cand, positive,
+    out, loss_out,
+    x0, x1, y, x2, flat, tw, tw_near, tw_far, tw_raw, q_raw, pre_out, pre_in, pre_own,
+    bias_raw, bias_cols, unit_raw, unit_cols, cands, users, targets, losses,
+    feat_sem, weight_sem, small_sem,
+    end_send, end_recv, cross_send, cross_recv, pair_send, pair_recv, one_send, one_recv,
+    piece_send, piece_recv, plane_send, plane_recv, tower_send, tower_recv, both_send, both_recv,
+    bias_send, bias_recv, unit_send, unit_recv, cand_send, cand_recv,
+    two_send, two_recv, out_sem, give_send, give_recv, part_send, part_recv, loss_send, loss_recv,
+):
+    batch_count, field_count, dim_count = counts
+    b = lax.axis_index("batch")
+    f = lax.axis_index("field")
+    d = lax.axis_index("dim")
+    members = field_count * dim_count
+    me = f * dim_count + d
+    chunks, fields, width, rc = x0.shape
+    fl, el, _ = feat.shape
+    wide = 2 * el
+    half_k = fields // 2 * width
+    quarter_units = tw_near.shape[0]
+    units = tw.shape[1]
+    side_k = fields * wide
+    lanes = rc // field_count
+    rows_in_part = el // 2
+    side = d // 2
+    mid = 1 + side
+    far = 2 - side
+    end = 3 * side
+    far_end = 3 - end
+    is_mid = d == mid
+    is_end = d == end
+    other = field_count - 1 - f
+    x_next = b + 1 - 2 * lax.rem(b, 2)
+    y_next = lax.rem(b + 2, 4)
+    diagonal = 3 - b
+    fs = pl.ds(f * fl, fl)
+    ss = pl.ds(pl.multiple_of(side * wide, wide), wide)
+
+    def remote(ref, send, recv, to=None, **where):
+        return pltpu.make_async_remote_copy(
+            ref, ref if to is None else to, send, recv, device_id=where, device_id_type=MESH)
+
+    def entries(o):
+        return pl.ds(pl.multiple_of(o * el, el), el)
+
+    def within(o):
+        return pl.ds(pl.multiple_of(lax.rem(o, 2) * el, el), el)
+
+    def block(c, ff, o):
+        return x0.at[c, pl.ds(ff * fl, fl), entries(o), :]
+
+    def from_end(c, target):
+        return remote(block(c, f, end), end_send.at[c], end_recv.at[c], dim=target)
+
+    def cross(k, c, o):
+        return remote(block(c, f, o), cross_send.at[k, c], cross_recv.at[k, c], dim=far)
+
+    def cross_one(c, s):
+        ref = x1.at[c, fs, pl.ds(pl.multiple_of(s * wide, wide), wide), :]
+        return remote(ref, cross_send.at[2, c], cross_recv.at[2, c], dim=far)
+
+    def pair(c, o, ff):
+        return remote(block(c, ff, o), pair_send.at[o, c], pair_recv.at[o, c], field=other)
+
+    def pair_one(c, s, ff):
+        ref = x1.at[c, pl.ds(ff * fl, fl), pl.ds(pl.multiple_of(s * wide, wide), wide), :]
+        return remote(ref, one_send.at[s, c], one_recv.at[s, c], field=other)
+
+    def weight_piece(level, p, source):
+        start, size = line_pieces(fl, PIECES)[p]
+        row = pl.multiple_of(lax.rem(end, 2) * el + lax.rem(source, 2) * rows_in_part, rows_in_part)
+        lane = pl.multiple_of(source // 2 * half_k, half_k)
+        return flat.at[level, pl.ds(start, size), pl.ds(row, rows_in_part), pl.ds(lane, half_k)]
+
+    def piece(level, p, target):
+        ref = weight_piece(level, p, b)
+        return remote(ref, piece_send.at[level, p], piece_recv.at[level, p], dim=target)
+
+    def tower_rows(member, source):
+        return tw.at[member, pl.ds(pl.multiple_of(source * quarter_units, quarter_units), quarter_units), :]
+
+    def item(i, source):
+        if i < CROSS * PIECES:
+            return weight_piece(i // PIECES, i % PIECES, source)
+        return tower_rows(f * dim_count + i - CROSS * PIECES, source)
+
+    def plane(i, slot, source, target):
+        return remote(item(i, source), plane_send.at[i, slot], plane_recv.at[i, source], batch=target)
+
+    def plane_out(i):
+        plane(i, 0, b, x_next).start()
+        plane(i, 1, b, y_next).start()
+
+    def relay(i):
+        return (x_next, y_next) if i % 2 == 0 else (y_next, x_next)
+
+    def plane_forward(i):
+        source, target = relay(i)
+        plane(i, 2, source, target).wait_recv()
+        plane(i, 2, source, target).start()
+
+    def plane_rest(i):
+        plane(i, 2, relay(i)[1], x_next).wait_recv()
+        plane(i, 2, diagonal, x_next).wait_recv()
+
+    def tower_item(z):
+        return CROSS * PIECES + z
+
+    def tower_copy(slot, ref, source, target):
+        return remote(
+            ref, tower_send.at[slot], tower_recv.at[source],
+            to=tower_rows(f * dim_count + source, b), dim=target)
+
+    def both(ff):
+        return remote(tw.at[pl.ds(ff * dim_count, dim_count)], both_send, both_recv, field=other)
+
+    def bias_copy(target):
+        return remote(bias_raw.at[lax.rem(end, 2)], bias_send, bias_recv, dim=target)
+
+    def unit_copy(k, source, ff, z):
+        return remote(unit_raw.at[source], unit_send.at[k], unit_recv.at[source], field=ff, dim=z)
+
+    def cand_copy(k, source):
+        t = lax.rem(b + k, batch_count)
+        return remote(cands.at[source], cand_send.at[k], cand_recv.at[source], batch=t)
+
+    def two(c, ff):
+        lane = pl.multiple_of((1 - ff) * lanes, lanes)
+        return remote(
+            y.at[c, :, :, pl.ds(lane, lanes)], two_send.at[c], two_recv.at[c],
+            to=x2.at[c, pl.ds(ff * fl, fl)], field=other)
+
+    def rows_of(c):
+        return pl.ds(pl.multiple_of(c * rc, rc), rc)
+
+    def keep(c):
+        return pltpu.make_async_copy(y.at[c, :, within(mid), :], out.at[:, :, rows_of(c)], out_sem.at[c])
+
+    def give(c):
+        return remote(
+            y.at[c, :, within(end), :], give_send.at[c], give_recv.at[c],
+            to=out.at[:, :, rows_of(c)], dim=end)
+
+    def part(j):
+        return remote(pre_out.at[j], part_send.at[j], part_recv.at[j], to=pre_in.at[j], dim=far)
+
+    def loss_copy(k, c, ff):
+        m = lax.rem(me + k, members)
+        return remote(
+            losses.at[c, ff], loss_send.at[c, k], loss_recv.at[c, ff],
+            field=m // dim_count, dim=lax.rem(m, dim_count))
+
+    def own_weight(level, ff):
+        return pltpu.make_async_copy(
+            weight.at[level, :, ff],
+            flat.at[level, :, within(mid), pl.ds(pl.multiple_of(ff * width, width), width)],
+            weight_sem.at[level, ff])
+
+    def end_weight(level, k):
+        row = pl.multiple_of(lax.rem(b, 2) * rows_in_part, rows_in_part)
+        ff = b // 2 * (fields // 2) + k
+        to = pl.multiple_of(lax.rem(end, 2) * el + row, rows_in_part)
+        return pltpu.make_async_copy(
+            weight.at[level, :, ff, pl.ds(row, rows_in_part), :],
+            flat.at[level, :, pl.ds(to, rows_in_part), pl.ds(pl.multiple_of(ff * width, width), width)],
+            weight_sem.at[level, k])
+
+    def each(count, act):
+        def step(k, carry):
+            act(k)
+            return carry
+
+        lax.fori_loop(0, count, step, 0)
+
+    own_features = [
+        pltpu.make_async_copy(feat.at[:, :, pl.ds(c * rc, rc)], block(c, f, d), feat_sem.at[c])
+        for c in range(chunks)]
+    quarter = pl.ds(pl.multiple_of(b * quarter_units, quarter_units), quarter_units)
+    small = [
+        pltpu.make_async_copy(bias, bias_raw.at[lax.rem(d, 2)], small_sem.at[0]),
+        pltpu.make_async_copy(tower_bias, unit_raw.at[me], small_sem.at[1]),
+        pltpu.make_async_copy(cand, cands.at[b], small_sem.at[2]),
+        pltpu.make_async_copy(tower.at[:, quarter, :], tw_raw, small_sem.at[3]),
+        pltpu.make_async_copy(query_weight.at[quarter, :], q_raw, small_sem.at[4]),
+        pltpu.make_async_copy(user, users, small_sem.at[5]),
+        pltpu.make_async_copy(positive, targets, small_sem.at[6]),
+    ]
+    for copy in own_features:
+        copy.start()
+
+    @pl.when(is_end)
+    def _():
+        each(fields // 2, lambda k: end_weight(0, k).start())
+
+    for copy in small:
+        copy.start()
+
+    @pl.when(is_mid)
+    def _():
+        each(fields, lambda k: own_weight(0, k).start())
+        each(fields, lambda k: own_weight(1, k).start())
+
+    @pl.when(is_end)
+    def _():
+        each(fields // 2, lambda k: end_weight(1, k).start())
+
+    barrier = pltpu.get_barrier_semaphore()
+    for k in range(1, members):
+        m = lax.rem(me + k, members)
+        pl.semaphore_signal(
+            barrier, inc=1, device_id={"field": m // dim_count, "dim": lax.rem(m, dim_count)},
+            device_id_type=MESH)
+    for k in range(1, batch_count):
+        pl.semaphore_signal(
+            barrier, inc=1, device_id={"batch": lax.rem(b + k, batch_count)}, device_id_type=MESH)
+    pl.semaphore_wait(barrier, members + batch_count - 2)
+
+    def unit_sends(act):
+        k = 0
+        for ff in range(field_count):
+            for z in (1, 2):
+                @pl.when((f != ff) | (d != z))
+                def _():
+                    act(unit_copy(k, me, ff, z))
+                k += 1
+
+    def pack_tower():
+        for s, ref in ((0, tw_near), (1, tw_far)):
+            start = jnp.where(s == 0, side, 1 - side)
+            for j in range(fields // 2):
+                first = tw_raw[2 * j]
+                second = tw_raw[2 * j + 1]
+                low = jnp.concatenate([first[:, :wide], second[:, :wide]], axis=1)
+                high = jnp.concatenate([first[:, wide:], second[:, wide:]], axis=1)
+                ref[:, j * width:(j + 1) * width] = jnp.where(start == 0, low, high)
+            ref[:, side_k:] = q_raw[...]
+
+    @pl.when(is_end)
+    def _():
+        each(fields // 2, lambda k: end_weight(0, k).wait())
+        piece(0, 0, mid).start()
+        piece(0, 1, mid).start()
+        for copy in own_features:
+            copy.wait()
+        from_end(0, mid).start()
+        piece(0, 2, mid).start()
+        piece(0, 3, mid).start()
+        for c in range(1, chunks):
+            from_end(c, mid).start()
+        for copy in small:
+            copy.wait()
+        bias_copy(mid).start()
+        unit_sends(lambda copy: copy.start())
+        pack_tower()
+        tower_copy(0, tw_near, d, mid).start()
+        tower_copy(1, tw_far, d, far).start()
+        each(fields // 2, lambda k: end_weight(1, k).wait())
+        for p in range(PIECES):
+            piece(1, p, mid).start()
+
+    def expect_piece(level, p):
+        piece(level, p, end).wait_recv()
+        plane_out(level * PIECES + p)
+
+    def expect_end(c):
+        from_end(c, end).wait_recv()
+        cross(1, c, end).start()
+        pair(c, end, f).start()
+
+    def expect_far(k, c, o):
+        cross(k, c, o).wait_recv()
+        pair(c, o, f).start()
+
+    def expect_tower(z):
+        tower_copy(0, tw_near, z, end).wait_recv()
+        for k in range(dim_count):
+            @pl.when(z == k)
+            def _():
+                plane_out(tower_item(k))
+
+    def on_tower(z, act):
+        for k in range(dim_count):
+            @pl.when(z == k)
+            def _():
+                act(tower_item(k))
+
+    def advance(source, level, c):
+        product = jnp.dot(
+            flat[level].reshape(fl * wide, fields * width), source[c].reshape(fields * width, rc),
+            preferred_element_type=jnp.float32)
+        column = bias_cols[level]
+        product = product + jnp.concatenate([column] * (rc // column.shape[1]), axis=1)
+        anchor = x0[c, fs, ss, :].astype(jnp.float32).reshape(fl * wide, rc)
+        current = source[c, fs, ss, :].astype(jnp.float32).reshape(fl * wide, rc)
+        return (anchor * product + current).astype(jnp.bfloat16).reshape(fl, wide, rc)
+
+    def build_bias():
+        pick = (lax.broadcasted_iota(jnp.int32, (el, el), 0) == lax.broadcasted_iota(jnp.int32, (el, el), 1))
+        for level in range(CROSS):
+            for k in range(fl):
+                for s in range(2):
+                    line = bias_raw[s, level, k:k + 1, :]
+                    column = jnp.sum(jnp.where(pick, line, 0.0), axis=1, keepdims=True)
+                    start = (2 * k + s) * el
+                    bias_cols[level, start:start + el, :] = jnp.broadcast_to(column, (el, width))
+
+    def build_units():
+        for m in range(members):
+            unit_cols[m * units:(m + 1) * units, :] = jnp.broadcast_to(unit_raw[m], (lanes, units)).T
+
+    def first(c, carry):
+        @pl.when(c == 1)
+        def _():
+            expect_end(3)
+
+        @pl.when(c == 2)
+        def _():
+            expect_far(1, 2, far_end)
+
+        @pl.when(c == 3)
+        def _():
+            expect_tower(end)
+            expect_far(1, 3, far_end)
+
+        for o in range(dim_count):
+            pair(c, o, other).wait_recv()
+        x1[c, fs, ss, :] = advance(x0, 0, c)
+        cross_one(c, side).start()
+        pair_one(c, side, f).start()
+        return carry
+
+    def tower_part(c):
+        matrix = tw[:, :, :side_k].reshape(members * units, side_k)
+        return jnp.dot(matrix, x2[c].reshape(side_k, lanes), preferred_element_type=jnp.float32)
+
+    def second(c, carry):
+        cross_one(c, 1 - side).wait_recv()
+        pair_one(c, 1 - side, f).start()
+        pair_one(c, side, other).wait_recv()
+        pair_one(c, 1 - side, other).wait_recv()
+        new = advance(x1, 1, c)
+        y[c] = new
+        two(c, f).start()
+        for ff in range(field_count):
+            @pl.when(f == ff)
+            def _():
+                x2[c, fs] = new[:, :, ff * lanes:(ff + 1) * lanes]
+        give(c).start()
+        keep(c).start()
+        two(c, other).wait_recv()
+        pre = tower_part(c)
+        j = c // 2
+
+        @pl.when(lax.rem(c, 2) == side)
+        def _():
+            pre_own[j] = pre
+
+        @pl.when(lax.rem(c, 2) != side)
+        def _():
+            pre_out[j] = pre.astype(jnp.bfloat16)
+            part(j).start()
+
+        return carry
+
+    def finish(j, carry):
+        c = 2 * j + side
+        part(j).wait_recv()
+        pre = pre_own[j] + pre_in[j].astype(jnp.float32) + unit_cols[...]
+        hidden = jnp.maximum(pre, 0.0).astype(jnp.bfloat16)
+        query = lax.dot_general(
+            hidden, tw[:, :, side_k:].reshape(members * units, width), (((0,), (0,)), ((), ())),
+            preferred_element_type=jnp.float32)
+        start = pl.multiple_of(c * rc + f * lanes, lanes)
+        query_vec = (query + users[pl.ds(start, lanes), :].astype(jnp.float32)).astype(jnp.bfloat16)
+        logits = lax.dot_general(
+            cands[...].reshape(-1, width), query_vec, (((1,), (1,)), ((), ())),
+            preferred_element_type=jnp.float32) * (1.0 / math.sqrt(width))
+        labels = lax.broadcasted_iota(jnp.int32, logits.shape, 0)
+        target = targets[c * field_count + f]
+        picked = jnp.sum(jnp.where(labels == target, logits, 0.0), axis=0, keepdims=True)
+        best = jnp.max(logits, axis=0, keepdims=True)
+        total = jnp.sum(jnp.exp(logits - best), axis=0, keepdims=True)
+        losses[c, f] = best + jnp.log(total) - picked
+        for k in range(1, members):
+            loss_copy(k, c, f).start()
+        return carry
+
+    @pl.when(is_mid)
+    def _():
+        for c in range(chunks):
+            own_features[c].wait()
+            cross(0, c, mid).start()
+            pair(c, mid, f).start()
+        for copy in small:
+            copy.wait()
+        unit_sends(lambda copy: copy.start())
+        for k in range(1, batch_count):
+            cand_copy(k, b).start()
+        pack_tower()
+        tower_copy(1, tw_far, d, far).start()
+        tw[me, quarter, :] = tw_near[...]
+        expect_piece(0, 0)
+        expect_far(0, 0, far)
+        expect_piece(0, 1)
+        plane_forward(0)
+        expect_far(0, 1, far)
+        expect_end(0)
+        plane_forward(1)
+        expect_far(0, 2, far)
+        expect_piece(0, 2)
+        expect_far(0, 3, far)
+        bias_copy(end).wait_recv()
+        build_bias()
+        expect_piece(0, 3)
+        plane_forward(2)
+        on_tower(d, plane_out)
+        expect_tower(far)
+        expect_end(1)
+        expect_far(1, 0, far_end)
+        plane_forward(3)
+        expect_end(2)
+        expect_far(1, 1, far_end)
+        for level in range(CROSS):
+            each(fields, lambda k: own_weight(level, k).wait())
+        for p in range(PIECES):
+            plane_rest(p)
+        lax.fori_loop(0, chunks, first, 0)
+        on_tower(d, plane_forward)
+        on_tower(far, plane_forward)
+        expect_piece(1, 0)
+        on_tower(end, plane_forward)
+        expect_tower(far_end)
+        expect_piece(1, 1)
+        plane_forward(PIECES)
+        on_tower(far_end, plane_forward)
+        expect_piece(1, 2)
+        plane_forward(PIECES + 1)
+        for k in range(1, batch_count):
+            cand_copy(0, lax.rem(b + k, batch_count)).wait_recv()
+        for m in range(members):
+            @pl.when(me != m)
+            def _():
+                unit_copy(0, m, f, d).wait_recv()
+        build_units()
+        for z in range(dim_count):
+            plane_rest(tower_item(z))
+        both(f).start()
+        expect_piece(1, 3)
+        plane_forward(PIECES + 2)
+        plane_forward(PIECES + 3)
+        for p in range(PIECES):
+            plane_rest(PIECES + p)
+        both(other).wait_recv()
+        lax.fori_loop(0, chunks, second, 0)
+        lax.fori_loop(0, chunks // 2, finish, 0)
+
+    for c in range(chunks):
+        for ff in range(field_count):
+            @pl.when(jnp.logical_not((d == 1 + c % 2) & (f == ff)))
+            def _():
+                loss_copy(1, c, ff).wait_recv()
+
+    for c in range(chunks):
+        for ff in range(field_count):
+            loss_out[c * field_count + ff] = losses[c, ff]
+
+    @pl.when(is_end)
+    def _():
+        for level in range(CROSS):
+            for p in range(PIECES):
+                piece(level, p, mid).wait_send()
+        for c in range(chunks):
+            from_end(c, mid).wait_send()
+            give(c).wait_recv()
+        bias_copy(mid).wait_send()
+        tower_copy(0, tw_near, d, mid).wait_send()
+        tower_copy(1, tw_far, d, far).wait_send()
+
+    unit_sends(lambda copy: copy.wait_send())
+
+    @pl.when(is_mid)
+    def _():
+        tower_copy(1, tw_far, d, far).wait_send()
+        for k in range(1, batch_count):
+            cand_copy(k, b).wait_send()
+        both(f).wait_send()
+
+        def drain(c, carry):
+            cross(0, c, mid).wait_send()
+            cross(1, c, end).wait_send()
+            cross_one(c, side).wait_send()
+            for o in range(dim_count):
+                pair(c, o, f).wait_send()
+            for s in range(2):
+                pair_one(c, s, f).wait_send()
+            two(c, f).wait_send()
+            give(c).wait_send()
+            keep(c).wait()
+            return carry
+
+        lax.fori_loop(0, chunks, drain, 0)
+
+        for i in range(CROSS * PIECES + dim_count):
+            plane(i, 0, b, x_next).wait_send()
+            plane(i, 1, b, y_next).wait_send()
+            plane(i, 2, *relay(i)).wait_send()
+
+        def drain_half(j, carry):
+            part(j).wait_send()
+            for k in range(1, members):
+                loss_copy(k, 2 * j + side, f).wait_send()
+            return carry
+
+        lax.fori_loop(0, chunks // 2, drain_half, 0)
+
+
+def line_body(
+    counts, features, cross_weight, cross_bias, tower_weight, tower_bias, query_weight,
+    user_vec, candidates, positive,
+):
+    batch_count, field_count, dim_count = counts
+    members = field_count * dim_count
+    fl, el, row_count = features.shape
+    units, fields, width = tower_weight.shape
+    rc = row_count // CHUNKS
+    lanes = rc // field_count
+    wide = 2 * el
+    quarter = units // batch_count
+    packed = fields * wide + width
+    pairs = CHUNKS // 2
+    items = CROSS * PIECES + dim_count
+    dma = pltpu.SemaphoreType.DMA
+    vmem = pltpu.VMEM
+    bf16 = jnp.bfloat16
+    f32 = jnp.float32
+    far = pl.BlockSpec(memory_space=pl.ANY)
+    near = pl.BlockSpec(memory_space=pltpu.VMEM)
+    crossed, losses = pl.pallas_call(
+        functools.partial(line_kernel, counts),
+        out_shape=(
+            jax.ShapeDtypeStruct(features.shape, bf16),
+            jax.ShapeDtypeStruct((CHUNKS * field_count, 1, lanes), f32),
+        ),
+        in_specs=[far] * 9,
+        out_specs=(far, near),
+        scratch_shapes=[
+            vmem((CHUNKS, fields, width, rc), bf16),
+            vmem((CHUNKS, fields, width, rc), bf16),
+            vmem((CHUNKS, fl, wide, rc), bf16),
+            vmem((CHUNKS, fields, wide, lanes), bf16),
+            vmem((CROSS, fl, wide, fields * width), bf16),
+            vmem((members, units, packed), bf16),
+            vmem((quarter, packed), bf16),
+            vmem((quarter, packed), bf16),
+            vmem((fields, quarter, width), bf16),
+            vmem((quarter, width), bf16),
+            vmem((pairs, members * units, lanes), bf16),
+            vmem((pairs, members * units, lanes), bf16),
+            vmem((pairs, members * units, lanes), f32),
+            vmem((2, CROSS, fl, el), f32),
+            vmem((CROSS, fl * wide, width), f32),
+            vmem((members, 1, units), f32),
+            vmem((members * units, lanes), f32),
+            vmem((batch_count,) + candidates.shape, bf16),
+            vmem(user_vec.shape, bf16),
+            vmem((CHUNKS * field_count, 1, lanes), jnp.int32),
+            vmem((CHUNKS, field_count, 1, lanes), f32),
+            dma((CHUNKS,)), dma((CROSS, fields)), dma((7,)),
+            dma((CHUNKS,)), dma((CHUNKS,)), dma((3, CHUNKS)), dma((3, CHUNKS)),
+            dma((dim_count, CHUNKS)), dma((dim_count, CHUNKS)), dma((2, CHUNKS)), dma((2, CHUNKS)),
+            dma((CROSS, PIECES)), dma((CROSS, PIECES)), dma((items, 3)), dma((items, batch_count)),
+            dma((2,)), dma((dim_count,)), dma, dma,
+            dma, dma, dma((members,)), dma((members,)), dma((batch_count,)), dma((batch_count,)),
+            dma((CHUNKS,)), dma((CHUNKS,)), dma((CHUNKS,)), dma((CHUNKS,)), dma((CHUNKS,)),
+            dma((pairs,)), dma((pairs,)), dma((CHUNKS, members)), dma((CHUNKS, field_count)),
+        ],
+        compiler_params=pltpu.CompilerParams(
+            collective_id=0, has_side_effects=True, vmem_limit_bytes=60 * 2**20),
+        name="line_forward",
+    )(
+        features,
+        cross_weight.transpose(0, 1, 3, 2, 4),
+        cross_bias,
+        tower_weight.transpose(1, 0, 2),
+        tower_bias.reshape(1, units),
+        query_weight,
+        user_vec,
+        candidates,
+        positive.reshape(CHUNKS * field_count, 1, lanes),
+    )
+    return (crossed, losses.reshape(row_count))
+
+
 def body(
     features, cross_weight, cross_bias, tower_weight, tower_bias, query_weight,
     user_vec, candidates, positive,
 ):
     counts = tuple(lax.axis_size(name) for name in ("batch", "field", "dim"))
+    if line_fits(counts, features, tower_weight, candidates):
+        return line_body(
+            counts, features, cross_weight, cross_bias, tower_weight, tower_bias, query_weight,
+            user_vec, candidates, positive)
     batch_count, field_count, dim_count = counts
     members = field_count * dim_count
     fl, el, row_count = features.shape

time: 154 us -> 156 us (1.013)
  Pallas kernels: 148 us -> 150 us
    pallas_call x1, Pallas kernels: 148 us -> 150 us  [line_body(): pl.pallas_call(functools.partial(line_kernel, counts), out_shape=(jax.Sha...]
where the time goes in v1:
time: 156 us
  Pallas kernels  150 us (96%)
  local copies, waits for them, and re-layouts  4.71 us (3%)
    pallas_call x1, Pallas kernels, line_body(): pl.pallas_call(functools.partial(line_kernel, counts), out_shape=(jax.Sha...  150 us
    unnamed x3, local copies, waits for them, and re-layouts  4.71 us

profile of v1, /device:TPU:0, one launch (start us, length us, event | category | flops | bytes accessed | tf_op | source)
XLA Modules:
  0.0 155.8 jit_solution(4181857163779670555)
XLA Ops:
  0.6 1.3 copy.11.bias
  1.9 150.5 %line_forward.1 = (bf16[13,32,1024]{2,1,0:T(8,128)(2,1)}, f32[8,1,128]{2,1,0:T(1,128)}) custom-call(bf16[13,32,1024]{2,1,0:T(8,128)(2,1)} %feat.1, bf16[2,13,26,32,128]{4,3,2,1,0:T(8,128)(2,1)} %bitcast.5, f32[2,13,32]{2,1,0:T(8,128)} %copy.11.bias, bf16[26,128,128]{2,1,0:T(8,128)(2,1)} %bitcast.6, f32[1,128]{1,0:T(1,128)} %bitcast.9, ...), custom_call_target="tpu_custom_call" | custom-call | tf_op jit(solution)/shard_map/line_forward/pallas_call | solution.py:989
  152.4 2.1 %copy.14 = bf16[13,32,1024]{2,1,0:T(8,128)(2,1)} copy(bf16[13,32,1024]{2,1,0:T(8,128)(2,1)} %get-tuple-element.8) | data formatting | bytes 1703936
  154.6 1.3 copy.15

commit v2 on v1

--- a/solution.py
+++ b/solution.py
@@ -444,6 +444,8 @@
 
 PIECES = 4
 CHUNKS = 4
+FAR_TOWER = CROSS * PIECES
+END_TOWER = FAR_TOWER + 1
 
 
 def line_kernel(
@@ -468,7 +470,7 @@
     fl, el, _ = feat.shape
     wide = 2 * el
     half_k = fields // 2 * width
-    quarter_units = tw_near.shape[0]
+    quarter_units = tw_far.shape[0]
     units = tw.shape[1]
     side_k = fields * wide
     lanes = rc // field_count
@@ -480,6 +482,8 @@
     far_end = 3 - end
     is_mid = d == mid
     is_end = d == end
+    owner = is_mid & (f == side)
+    giver = is_mid & (f != side)
     other = field_count - 1 - f
     x_next = b + 1 - 2 * lax.rem(b, 2)
     y_next = lax.rem(b + 2, 4)
@@ -533,7 +537,7 @@
     def item(i, source):
         if i < CROSS * PIECES:
             return weight_piece(i // PIECES, i % PIECES, source)
-        return tower_rows(f * dim_count + i - CROSS * PIECES, source)
+        return tower_rows(f * dim_count + (far if i == FAR_TOWER else far_end), source)
 
     def plane(i, slot, source, target):
         return remote(item(i, source), plane_send.at[i, slot], plane_recv.at[i, source], batch=target)
@@ -554,16 +558,17 @@
         plane(i, 2, relay(i)[1], x_next).wait_recv()
         plane(i, 2, diagonal, x_next).wait_recv()
 
-    def tower_item(z):
-        return CROSS * PIECES + z
-
-    def tower_copy(slot, ref, source, target):
+    def near_tower(target):
         return remote(
-            ref, tower_send.at[slot], tower_recv.at[source],
+            tw_near, tower_send.at[0], tower_recv.at[end], to=tw.at[f * dim_count + end], dim=target)
+
+    def far_tower(source, target):
+        return remote(
+            tw_far, tower_send.at[1], tower_recv.at[source],
             to=tower_rows(f * dim_count + source, b), dim=target)
 
-    def both(ff):
-        return remote(tw.at[pl.ds(ff * dim_count, dim_count)], both_send, both_recv, field=other)
+    def both(z, ff):
+        return remote(tw.at[ff * dim_count + z], both_send.at[z], both_recv.at[z], field=other)
 
     def bias_copy(target):
         return remote(bias_raw.at[lax.rem(end, 2)], bias_send, bias_recv, dim=target)
@@ -592,8 +597,8 @@
             y.at[c, :, within(end), :], give_send.at[c], give_recv.at[c],
             to=out.at[:, :, rows_of(c)], dim=end)
 
-    def part(j):
-        return remote(pre_out.at[j], part_send.at[j], part_recv.at[j], to=pre_in.at[j], dim=far)
+    def part(c):
+        return remote(pre_out.at[c], part_send.at[c], part_recv.at[c], to=pre_in.at[c], dim=far)
 
     def loss_copy(k, c, ff):
         m = lax.rem(me + k, members)
@@ -631,8 +636,8 @@
         pltpu.make_async_copy(bias, bias_raw.at[lax.rem(d, 2)], small_sem.at[0]),
         pltpu.make_async_copy(tower_bias, unit_raw.at[me], small_sem.at[1]),
         pltpu.make_async_copy(cand, cands.at[b], small_sem.at[2]),
-        pltpu.make_async_copy(tower.at[:, quarter, :], tw_raw, small_sem.at[3]),
-        pltpu.make_async_copy(query_weight.at[quarter, :], q_raw, small_sem.at[4]),
+        pltpu.make_async_copy(tower, tw_raw, small_sem.at[3]),
+        pltpu.make_async_copy(query_weight, q_raw, small_sem.at[4]),
         pltpu.make_async_copy(user, users, small_sem.at[5]),
         pltpu.make_async_copy(positive, targets, small_sem.at[6]),
     ]
@@ -676,38 +681,44 @@
                 k += 1
 
     def pack_tower():
-        for s, ref in ((0, tw_near), (1, tw_far)):
-            start = jnp.where(s == 0, side, 1 - side)
-            for j in range(fields // 2):
-                first = tw_raw[2 * j]
-                second = tw_raw[2 * j + 1]
-                low = jnp.concatenate([first[:, :wide], second[:, :wide]], axis=1)
-                high = jnp.concatenate([first[:, wide:], second[:, wide:]], axis=1)
-                ref[:, j * width:(j + 1) * width] = jnp.where(start == 0, low, high)
-            ref[:, side_k:] = q_raw[...]
+        def halves(rows, j):
+            first = tw_raw[2 * j, rows, :]
+            second = tw_raw[2 * j + 1, rows, :]
+            low = jnp.concatenate([first[:, :wide], second[:, :wide]], axis=1)
+            high = jnp.concatenate([first[:, wide:], second[:, wide:]], axis=1)
+            return low, high
+
+        for j in range(fields // 2):
+            low, high = halves(slice(None), j)
+            tw_near[:, j * width:(j + 1) * width] = jnp.where(side == 0, low, high)
+            low, high = halves(quarter, j)
+            tw_far[:, j * width:(j + 1) * width] = jnp.where(side == 0, high, low)
+        tw_near[:, side_k:] = q_raw[...]
+        tw_far[:, side_k:] = q_raw[quarter, :]
 
     @pl.when(is_end)
     def _():
+        small[0].wait()
+        bias_copy(mid).start()
+        small[1].wait()
+        unit_sends(lambda copy: copy.start())
         each(fields // 2, lambda k: end_weight(0, k).wait())
-        piece(0, 0, mid).start()
-        piece(0, 1, mid).start()
-        for copy in own_features:
+        for p in range(PIECES - 1):
+            piece(0, p, mid).start()
+        own_features[0].wait()
+        from_end(0, mid).start()
+        piece(0, PIECES - 1, mid).start()
+        for c in range(1, chunks):
+            own_features[c].wait()
+            from_end(c, mid).start()
+        for copy in small[2:]:
             copy.wait()
-        from_end(0, mid).start()
-        piece(0, 2, mid).start()
-        piece(0, 3, mid).start()
-        for c in range(1, chunks):
-            from_end(c, mid).start()
-        for copy in small:
-            copy.wait()
-        bias_copy(mid).start()
-        unit_sends(lambda copy: copy.start())
         pack_tower()
-        tower_copy(0, tw_near, d, mid).start()
-        tower_copy(1, tw_far, d, far).start()
+        far_tower(d, far).start()
         each(fields // 2, lambda k: end_weight(1, k).wait())
         for p in range(PIECES):
             piece(1, p, mid).start()
+        near_tower(mid).start()
 
     def expect_piece(level, p):
         piece(level, p, end).wait_recv()
@@ -722,23 +733,20 @@
         cross(k, c, o).wait_recv()
         pair(c, o, f).start()
 
-    def expect_tower(z):
-        tower_copy(0, tw_near, z, end).wait_recv()
-        for k in range(dim_count):
-            @pl.when(z == k)
-            def _():
-                plane_out(tower_item(k))
-
-    def on_tower(z, act):
-        for k in range(dim_count):
-            @pl.when(z == k)
-            def _():
-                act(tower_item(k))
-
-    def advance(source, level, c):
-        product = jnp.dot(
-            flat[level].reshape(fl * wide, fields * width), source[c].reshape(fields * width, rc),
+    def expect_tower(i, z):
+        far_tower(z, end).wait_recv()
+        plane_out(i)
+
+    def half(source, level, c, ff):
+        matrix = flat[level, :, :, pl.ds(pl.multiple_of(ff * half_k, half_k), half_k)]
+        return jnp.dot(
+            matrix.reshape(fl * wide, half_k), source[c, pl.ds(ff * fl, fl)].reshape(half_k, rc),
             preferred_element_type=jnp.float32)
+
+    def advance(source, level, c, wait_pair):
+        product = half(source, level, c, f)
+        wait_pair()
+        product = product + half(source, level, c, other)
         column = bias_cols[level]
         product = product + jnp.concatenate([column] * (rc // column.shape[1]), axis=1)
         anchor = x0[c, fs, ss, :].astype(jnp.float32).reshape(fl * wide, rc)
@@ -750,7 +758,7 @@
         for level in range(CROSS):
             for k in range(fl):
                 for s in range(2):
-                    line = bias_raw[s, level, k:k + 1, :]
+                    line = bias_raw[s, k, level:level + 1, :]
                     column = jnp.sum(jnp.where(pick, line, 0.0), axis=1, keepdims=True)
                     start = (2 * k + s) * el
                     bias_cols[level, start:start + el, :] = jnp.broadcast_to(column, (el, width))
@@ -763,60 +771,84 @@
         @pl.when(c == 1)
         def _():
             expect_end(3)
+            cross_one(0, side).start()
 
         @pl.when(c == 2)
         def _():
+            plane_forward(FAR_TOWER)
             expect_far(1, 2, far_end)
 
         @pl.when(c == 3)
         def _():
-            expect_tower(end)
+            expect_tower(END_TOWER, far_end)
             expect_far(1, 3, far_end)
-
-        for o in range(dim_count):
-            pair(c, o, other).wait_recv()
-        x1[c, fs, ss, :] = advance(x0, 0, c)
-        cross_one(c, side).start()
+            expect_piece(1, 0)
+
+        def wait_pair():
+            for o in range(dim_count):
+                pair(c, o, other).wait_recv()
+
+        x1[c, fs, ss, :] = advance(x0, 0, c, wait_pair)
         pair_one(c, side, f).start()
+
+        @pl.when(c > 0)
+        def _():
+            cross_one(c, side).start()
+
         return carry
 
     def tower_part(c):
         matrix = tw[:, :, :side_k].reshape(members * units, side_k)
         return jnp.dot(matrix, x2[c].reshape(side_k, lanes), preferred_element_type=jnp.float32)
 
-    def second(c, carry):
+    def layer_two(c):
         cross_one(c, 1 - side).wait_recv()
         pair_one(c, 1 - side, f).start()
-        pair_one(c, side, other).wait_recv()
-        pair_one(c, 1 - side, other).wait_recv()
-        new = advance(x1, 1, c)
-        y[c] = new
+
+        def wait_pair():
+            pair_one(c, side, other).wait_recv()
+            pair_one(c, 1 - side, other).wait_recv()
+
+        y[c] = advance(x1, 1, c, wait_pair)
         two(c, f).start()
+        give(c).start()
+        keep(c).start()
         for ff in range(field_count):
             @pl.when(f == ff)
             def _():
-                x2[c, fs] = new[:, :, ff * lanes:(ff + 1) * lanes]
-        give(c).start()
-        keep(c).start()
+                x2[c, fs] = y[c, :, :, ff * lanes:(ff + 1) * lanes]
+
+    def layer_three(c):
         two(c, other).wait_recv()
         pre = tower_part(c)
-        j = c // 2
-
-        @pl.when(lax.rem(c, 2) == side)
-        def _():
-            pre_own[j] = pre
-
-        @pl.when(lax.rem(c, 2) != side)
-        def _():
-            pre_out[j] = pre.astype(jnp.bfloat16)
-            part(j).start()
+
+        @pl.when(owner)
+        def _():
+            pre_own[c] = pre
+
+        @pl.when(giver)
+        def _():
+            pre_out[c] = pre.astype(jnp.bfloat16)
+            part(c).start()
+
+    def second(c, carry):
+        @pl.when(c < chunks)
+        def _():
+            layer_two(c)
+
+        @pl.when(c > 0)
+        def _():
+            layer_three(c - 1)
+
+        @pl.when(owner & (c > 1))
+        def _():
+            finish(c - 2)
 
         return carry
 
-    def finish(j, carry):
-        c = 2 * j + side
-        part(j).wait_recv()
-        pre = pre_own[j] + pre_in[j].astype(jnp.float32) + unit_cols[...]
+    def finish(c):
+        part(c).wait_recv()
+        pre = pre_own[c] + pre_in[c].astype(jnp.float32) + unit_cols[...]
         hidden = jnp.maximum(pre, 0.0).astype(jnp.bfloat16)
         query = lax.dot_general(
             hidden, tw[:, :, side_k:].reshape(members * units, width), (((0,), (0,)), ((), ())),
@@ -834,7 +866,6 @@
         losses[c, f] = best + jnp.log(total) - picked
         for k in range(1, members):
             loss_copy(k, c, f).start()
-        return carry
 
     @pl.when(is_mid)
     def _():
@@ -842,50 +873,42 @@
             own_features[c].wait()
             cross(0, c, mid).start()
             pair(c, mid, f).start()
-        for copy in small:
+        small[1].wait()
+        unit_sends(lambda copy: copy.start())
+        for copy in small[:1] + small[2:]:
             copy.wait()
-        unit_sends(lambda copy: copy.start())
         for k in range(1, batch_count):
             cand_copy(k, b).start()
         pack_tower()
-        tower_copy(1, tw_far, d, far).start()
-        tw[me, quarter, :] = tw_near[...]
+        far_tower(d, far).start()
+        tw[me] = tw_near[...]
+        both(mid, f).start()
+        bias_copy(end).wait_recv()
+        build_bias()
         expect_piece(0, 0)
         expect_far(0, 0, far)
         expect_piece(0, 1)
+        expect_far(0, 1, far)
         plane_forward(0)
-        expect_far(0, 1, far)
+        expect_piece(0, 2)
+        expect_far(0, 2, far)
+        plane_forward(1)
         expect_end(0)
-        plane_forward(1)
-        expect_far(0, 2, far)
-        expect_piece(0, 2)
         expect_far(0, 3, far)
-        bias_copy(end).wait_recv()
-        build_bias()
+        plane_forward(2)
+        expect_tower(FAR_TOWER, far)
         expect_piece(0, 3)
-        plane_forward(2)
-        on_tower(d, plane_out)
-        expect_tower(far)
+        expect_far(1, 0, far_end)
         expect_end(1)
-        expect_far(1, 0, far_end)
         plane_forward(3)
-        expect_end(2)
-        expect_far(1, 1, far_end)
         for level in range(CROSS):
             each(fields, lambda k: own_weight(level, k).wait())
+        expect_end(2)
         for p in range(PIECES):
             plane_rest(p)
+        expect_far(1, 1, far_end)
         lax.fori_loop(0, chunks, first, 0)
-        on_tower(d, plane_forward)
-        on_tower(far, plane_forward)
-        expect_piece(1, 0)
-        on_tower(end, plane_forward)
-        expect_tower(far_end)
-        expect_piece(1, 1)
-        plane_forward(PIECES)
-        on_tower(far_end, plane_forward)
-        expect_piece(1, 2)
-        plane_forward(PIECES + 1)
+        plane_forward(END_TOWER)
         for k in range(1, batch_count):
             cand_copy(0, lax.rem(b + k, batch_count)).wait_recv()
         for m in range(members):
@@ -893,21 +916,31 @@
             def _():
                 unit_copy(0, m, f, d).wait_recv()
         build_units()
-        for z in range(dim_count):
-            plane_rest(tower_item(z))
-        both(f).start()
+        expect_piece(1, 1)
+        plane_forward(PIECES)
+        expect_piece(1, 2)
+        plane_forward(PIECES + 1)
         expect_piece(1, 3)
+        for i, z in ((FAR_TOWER, far), (END_TOWER, far_end)):
+            plane_rest(i)
+            both(z, f).start()
         plane_forward(PIECES + 2)
         plane_forward(PIECES + 3)
+        near_tower(end).wait_recv()
+        both(end, f).start()
         for p in range(PIECES):
             plane_rest(PIECES + p)
-        both(other).wait_recv()
-        lax.fori_loop(0, chunks, second, 0)
-        lax.fori_loop(0, chunks // 2, finish, 0)
+        for z in range(dim_count):
+            both(z, other).wait_recv()
+        lax.fori_loop(0, chunks + 1, second, 0)
+
+        @pl.when(owner)
+        def _():
+            finish(chunks - 1)
 
     for c in range(chunks):
         for ff in range(field_count):
-            @pl.when(jnp.logical_not((d == 1 + c % 2) & (f == ff)))
+            @pl.when(jnp.logical_not((d == 1 + ff) & (f == ff)))
             def _():
                 loss_copy(1, c, ff).wait_recv()
 
@@ -924,17 +957,18 @@
             from_end(c, mid).wait_send()
             give(c).wait_recv()
         bias_copy(mid).wait_send()
-        tower_copy(0, tw_near, d, mid).wait_send()
-        tower_copy(1, tw_far, d, far).wait_send()
+        near_tower(mid).wait_send()
+        far_tower(d, far).wait_send()
 
     unit_sends(lambda copy: copy.wait_send())
 
     @pl.when(is_mid)
     def _():
-        tower_copy(1, tw_far, d, far).wait_send()
+        far_tower(d, far).wait_send()
         for k in range(1, batch_count):
             cand_copy(k, b).wait_send()
-        both(f).wait_send()
+        for z in range(dim_count):
+            both(z, f).wait_send()
 
         def drain(c, carry):
             cross(0, c, mid).wait_send()
@@ -951,18 +985,24 @@
 
         lax.fori_loop(0, chunks, drain, 0)
 
-        for i in range(CROSS * PIECES + dim_count):
+        for i in range(END_TOWER + 1):
             plane(i, 0, b, x_next).wait_send()
             plane(i, 1, b, y_next).wait_send()
             plane(i, 2, *relay(i)).wait_send()
 
-        def drain_half(j, carry):
-            part(j).wait_send()
+    @pl.when(giver)
+    def _():
+        for c in range(chunks):
+            part(c).wait_send()
+
+    @pl.when(owner)
+    def _():
+        def drain_losses(c, carry):
             for k in range(1, members):
-                loss_copy(k, 2 * j + side, f).wait_send()
+                loss_copy(k, c, f).wait_send()
             return carry
 
-        lax.fori_loop(0, chunks // 2, drain_half, 0)
+        lax.fori_loop(0, chunks, drain_losses, 0)
 
 
 def line_body(
@@ -978,8 +1018,7 @@
     wide = 2 * el
     quarter = units // batch_count
     packed = fields * wide + width
-    pairs = CHUNKS // 2
-    items = CROSS * PIECES + dim_count
+    items = END_TOWER + 1
     dma = pltpu.SemaphoreType.DMA
     vmem = pltpu.VMEM
     bf16 = jnp.bfloat16
@@ -1001,14 +1040,14 @@
             vmem((CHUNKS, fields, wide, lanes), bf16),
             vmem((CROSS, fl, wide, fields * width), bf16),
             vmem((members, units, packed), bf16),
+            vmem((units, packed), bf16),
             vmem((quarter, packed), bf16),
-            vmem((quarter, packed), bf16),
-            vmem((fields, quarter, width), bf16),
-            vmem((quarter, width), bf16),
-            vmem((pairs, members * units, lanes), bf16),
-            vmem((pairs, members * units, lanes), bf16),
-            vmem((pairs, members * units, lanes), f32),
-            vmem((2, CROSS, fl, el), f32),
+            vmem((fields, units, width), bf16),
+            vmem((units, width), bf16),
+            vmem((CHUNKS, members * units, lanes), bf16),
+            vmem((CHUNKS, members * units, lanes), bf16),
+            vmem((CHUNKS, members * units, lanes), f32),
+            vmem((2, fl, CROSS, el), f32),
             vmem((CROSS, fl * wide, width), f32),
             vmem((members, 1, units), f32),
             vmem((members * units, lanes), f32),
@@ -1020,10 +1059,10 @@
             dma((CHUNKS,)), dma((CHUNKS,)), dma((3, CHUNKS)), dma((3, CHUNKS)),
             dma((dim_count, CHUNKS)), dma((dim_count, CHUNKS)), dma((2, CHUNKS)), dma((2, CHUNKS)),
             dma((CROSS, PIECES)), dma((CROSS, PIECES)), dma((items, 3)), dma((items, batch_count)),
-            dma((2,)), dma((dim_count,)), dma, dma,
+            dma((2,)), dma((dim_count,)), dma((dim_count,)), dma((dim_count,)),
             dma, dma, dma((members,)), dma((members,)), dma((batch_count,)), dma((batch_count,)),
             dma((CHUNKS,)), dma((CHUNKS,)), dma((CHUNKS,)), dma((CHUNKS,)), dma((CHUNKS,)),
-            dma((pairs,)), dma((pairs,)), dma((CHUNKS, members)), dma((CHUNKS, field_count)),
+            dma((CHUNKS,)), dma((CHUNKS,)), dma((CHUNKS, members)), dma((CHUNKS, field_count)),
         ],
         compiler_params=pltpu.CompilerParams(
             collective_id=0, has_side_effects=True, vmem_limit_bytes=60 * 2**20),
@@ -1031,7 +1070,7 @@
     )(
         features,
         cross_weight.transpose(0, 1, 3, 2, 4),
-        cross_bias,
+        cross_bias.transpose(1, 0, 2),
         tower_weight.transpose(1, 0, 2),
         tower_bias.reshape(1, units),
         query_weight,

time: 156 us -> 118 us (0.76)
  Pallas kernels: 150 us -> 114 us
    pallas_call x1, Pallas kernels: 150 us -> 114 us  [line_body(): pl.pallas_call(functools.partial(line_kernel, counts), out_shape=(jax.Sha...]
    unnamed x3 -> x2, local copies, waits for them, and re-layouts: 4.71 us -> 3.39 us
where the time goes in v2:
time: 118 us
  Pallas kernels  114 us (97%)
  local copies, waits for them, and re-layouts  3.39 us (3%)
    pallas_call x1, Pallas kernels, line_body(): pl.pallas_call(functools.partial(line_kernel, counts), out_shape=(jax.Sha...  114 us
    unnamed x2, local copies, waits for them, and re-layouts  3.39 us

profile of v2, /device:TPU:0, one launch (start us, length us, event | category | flops | bytes accessed | tf_op | source)
XLA Modules:
  0.0 117.6 jit_solution(8236259727387942837)
XLA Ops:
  0.6 113.6 %line_forward.1 = (bf16[13,32,1024]{2,1,0:T(8,128)(2,1)}, f32[8,1,128]{2,1,0:T(1,128)}) custom-call(bf16[13,32,1024]{2,1,0:T(8,128)(2,1)} %feat.1, bf16[2,13,26,32,128]{4,3,2,1,0:T(8,128)(2,1)} %bitcast.6, f32[13,2,32]{2,1,0:T(2,128)} %bitcast.8, bf16[26,128,128]{2,1,0:T(8,128)(2,1)} %bitcast.7, f32[1,128]{1,0:T(1,128)} %bitcast.11, ...), custom_call_target="tpu_custom_call" | custom-call | tf_op jit(solution)/shard_map/line_forward/pallas_call | solution.py:1028
  114.2 2.1 %copy.13 = bf16[13,32,1024]{2,1,0:T(8,128)(2,1)} copy(bf16[13,32,1024]{2,1,0:T(8,128)(2,1)} %get-tuple-element.8) | data formatting | bytes 1703936
  116.4 1.3 %copy.14 = f32[1024]{0:T(1024)} copy(f32[1024]{0:T(1024)} %bitcast.10) | data formatting | bytes 8192

commit v3 on v2

--- a/solution.py
+++ b/solution.py
@@ -456,7 +456,8 @@
     bias_raw, bias_cols, unit_raw, unit_cols, cands, users, targets, losses,
     feat_sem, weight_sem, small_sem,
     end_send, end_recv, cross_send, cross_recv, pair_send, pair_recv, one_send, one_recv,
-    piece_send, piece_recv, plane_send, plane_recv, tower_send, tower_recv, both_send, both_recv,
+    piece_send, piece_recv, plane_send, plane_recv, rest_recv,
+    tower_send, tower_recv, both_send, both_recv,
     bias_send, bias_recv, unit_send, unit_recv, cand_send, cand_recv,
     two_send, two_recv, out_sem, give_send, give_recv, part_send, part_recv, loss_send, loss_recv,
 ):
@@ -495,6 +496,12 @@
         return pltpu.make_async_remote_copy(
             ref, ref if to is None else to, send, recv, device_id=where, device_id_type=MESH)
 
+    def sent(ref, sem):
+        remote(ref, sem, sem, field=other).wait_send()
+
+    def landed(ref, sem):
+        remote(ref, sem, sem, field=other).wait_recv()
+
     def entries(o):
         return pl.ds(pl.multiple_of(o * el, el), el)
 
@@ -505,31 +512,34 @@
         return x0.at[c, pl.ds(ff * fl, fl), entries(o), :]
 
     def from_end(c, target):
-        return remote(block(c, f, end), end_send.at[c], end_recv.at[c], dim=target)
+        return remote(block(c, f, end), end_send, end_recv.at[c], dim=target)
 
     def cross(k, c, o):
-        return remote(block(c, f, o), cross_send.at[k, c], cross_recv.at[k, c], dim=far)
+        return remote(block(c, f, o), cross_send.at[k], cross_recv.at[k, c], dim=far)
 
     def cross_one(c, s):
         ref = x1.at[c, fs, pl.ds(pl.multiple_of(s * wide, wide), wide), :]
-        return remote(ref, cross_send.at[2, c], cross_recv.at[2, c], dim=far)
-
-    def pair(c, o, ff):
-        return remote(block(c, ff, o), pair_send.at[o, c], pair_recv.at[o, c], field=other)
-
-    def pair_one(c, s, ff):
-        ref = x1.at[c, pl.ds(ff * fl, fl), pl.ds(pl.multiple_of(s * wide, wide), wide), :]
-        return remote(ref, one_send.at[s, c], one_recv.at[s, c], field=other)
+        return remote(ref, cross_send.at[2], cross_recv.at[2, c], dim=far)
+
+    def pair(c, o):
+        return remote(block(c, f, o), pair_send, pair_recv.at[c], field=other)
+
+    def pair_one(c, s):
+        ref = x1.at[c, fs, pl.ds(pl.multiple_of(s * wide, wide), wide), :]
+        return remote(ref, one_send, one_recv.at[c], field=other)
 
     def weight_piece(level, p, source):
         start, size = line_pieces(fl, PIECES)[p]
+        return weight_part(level, start, size, source)
+
+    def weight_part(level, start, size, source):
         row = pl.multiple_of(lax.rem(end, 2) * el + lax.rem(source, 2) * rows_in_part, rows_in_part)
         lane = pl.multiple_of(source // 2 * half_k, half_k)
         return flat.at[level, pl.ds(start, size), pl.ds(row, rows_in_part), pl.ds(lane, half_k)]
 
     def piece(level, p, target):
         ref = weight_piece(level, p, b)
-        return remote(ref, piece_send.at[level, p], piece_recv.at[level, p], dim=target)
+        return remote(ref, piece_send.at[level], piece_recv.at[level, p], dim=target)
 
     def tower_rows(member, source):
         return tw.at[member, pl.ds(pl.multiple_of(source * quarter_units, quarter_units), quarter_units), :]
@@ -539,24 +549,30 @@
             return weight_piece(i // PIECES, i % PIECES, source)
         return tower_rows(f * dim_count + (far if i == FAR_TOWER else far_end), source)
 
-    def plane(i, slot, source, target):
-        return remote(item(i, source), plane_send.at[i, slot], plane_recv.at[i, source], batch=target)
-
-    def plane_out(i):
-        plane(i, 0, b, x_next).start()
-        plane(i, 1, b, y_next).start()
-
     def relay(i):
         return (x_next, y_next) if i % 2 == 0 else (y_next, x_next)
 
+    def plane(i, source, target, arrival):
+        group = i // PIECES
+        return remote(item(i, source), plane_send.at[group], arrival, batch=target)
+
+    def plane_out(i):
+        first, second = relay(i)
+        plane(i, b, first, plane_recv.at[i]).start()
+        plane(i, b, second, rest_recv.at[i // PIECES]).start()
+
     def plane_forward(i):
         source, target = relay(i)
-        plane(i, 2, source, target).wait_recv()
-        plane(i, 2, source, target).start()
-
-    def plane_rest(i):
-        plane(i, 2, relay(i)[1], x_next).wait_recv()
-        plane(i, 2, diagonal, x_next).wait_recv()
+        plane(i, source, target, plane_recv.at[i]).wait_recv()
+        plane(i, source, target, rest_recv.at[i // PIECES]).start()
+
+    def plane_rest(group):
+        landed(plane_bytes(group, 2), rest_recv.at[group])
+
+    def plane_bytes(group, copies):
+        if group < CROSS:
+            return flat.at[group, :, pl.ds(0, copies * rows_in_part), pl.ds(0, half_k)]
+        return tw.at[pl.ds(0, copies * 2), pl.ds(0, quarter_units), :]
 
     def near_tower(target):
         return remote(
@@ -568,49 +584,48 @@
             to=tower_rows(f * dim_count + source, b), dim=target)
 
     def both(z, ff):
-        return remote(tw.at[ff * dim_count + z], both_send.at[z], both_recv.at[z], field=other)
+        return remote(tw.at[ff * dim_count + z], both_send, both_recv, field=other)
 
     def bias_copy(target):
         return remote(bias_raw.at[lax.rem(end, 2)], bias_send, bias_recv, dim=target)
 
-    def unit_copy(k, source, ff, z):
-        return remote(unit_raw.at[source], unit_send.at[k], unit_recv.at[source], field=ff, dim=z)
-
-    def cand_copy(k, source):
-        t = lax.rem(b + k, batch_count)
-        return remote(cands.at[source], cand_send.at[k], cand_recv.at[source], batch=t)
+    def unit_copy(ff, z):
+        return remote(unit_raw.at[me], unit_send, unit_recv, field=ff, dim=z)
+
+    def cand_copy(k):
+        return remote(cands.at[b], cand_send, cand_recv, batch=lax.rem(b + k, batch_count))
 
     def two(c, ff):
         lane = pl.multiple_of((1 - ff) * lanes, lanes)
         return remote(
-            y.at[c, :, :, pl.ds(lane, lanes)], two_send.at[c], two_recv.at[c],
+            y.at[c, :, :, pl.ds(lane, lanes)], two_send, two_recv.at[c],
             to=x2.at[c, pl.ds(ff * fl, fl)], field=other)
 
     def rows_of(c):
         return pl.ds(pl.multiple_of(c * rc, rc), rc)
 
     def keep(c):
-        return pltpu.make_async_copy(y.at[c, :, within(mid), :], out.at[:, :, rows_of(c)], out_sem.at[c])
+        return pltpu.make_async_copy(y.at[c, :, within(mid), :], out.at[:, :, rows_of(c)], out_sem)
 
     def give(c):
         return remote(
-            y.at[c, :, within(end), :], give_send.at[c], give_recv.at[c],
+            y.at[c, :, within(end), :], give_send, give_recv,
             to=out.at[:, :, rows_of(c)], dim=end)
 
     def part(c):
-        return remote(pre_out.at[c], part_send.at[c], part_recv.at[c], to=pre_in.at[c], dim=far)
-
-    def loss_copy(k, c, ff):
+        return remote(pre_out.at[c], part_send, part_recv.at[c], to=pre_in.at[c], dim=far)
+
+    def loss_copy(k, c):
         m = lax.rem(me + k, members)
         return remote(
-            losses.at[c, ff], loss_send.at[c, k], loss_recv.at[c, ff],
+            losses.at[f, c], loss_send.at[k], loss_recv,
             field=m // dim_count, dim=lax.rem(m, dim_count))
 
     def own_weight(level, ff):
         return pltpu.make_async_copy(
             weight.at[level, :, ff],
             flat.at[level, :, within(mid), pl.ds(pl.multiple_of(ff * width, width), width)],
-            weight_sem.at[level, ff])
+            weight_sem.at[level])
 
     def end_weight(level, k):
         row = pl.multiple_of(lax.rem(b, 2) * rows_in_part, rows_in_part)
@@ -619,7 +634,7 @@
         return pltpu.make_async_copy(
             weight.at[level, :, ff, pl.ds(row, rows_in_part), :],
             flat.at[level, :, pl.ds(to, rows_in_part), pl.ds(pl.multiple_of(ff * width, width), width)],
-            weight_sem.at[level, k])
+            weight_sem.at[level])
 
     def each(count, act):
         def step(k, carry):
@@ -671,14 +686,20 @@
             barrier, inc=1, device_id={"batch": lax.rem(b + k, batch_count)}, device_id_type=MESH)
     pl.semaphore_wait(barrier, members + batch_count - 2)
 
-    def unit_sends(act):
-        k = 0
+    def unit_sends():
         for ff in range(field_count):
             for z in (1, 2):
                 @pl.when((f != ff) | (d != z))
                 def _():
-                    act(unit_copy(k, me, ff, z))
-                k += 1
+                    unit_copy(ff, z).start()
+
+    def loaded_own(level):
+        ref = flat.at[level, :, within(mid), :]
+        pltpu.make_async_copy(ref, ref, weight_sem.at[level]).wait()
+
+    def loaded_end(level):
+        ref = weight_part(level, 0, fl, b)
+        pltpu.make_async_copy(ref, ref, weight_sem.at[level]).wait()
 
     def pack_tower():
         def halves(rows, j):
@@ -698,27 +719,26 @@
 
     @pl.when(is_end)
     def _():
-        small[0].wait()
-        bias_copy(mid).start()
-        small[1].wait()
-        unit_sends(lambda copy: copy.start())
-        each(fields // 2, lambda k: end_weight(0, k).wait())
+        loaded_end(0)
         for p in range(PIECES - 1):
             piece(0, p, mid).start()
-        own_features[0].wait()
-        from_end(0, mid).start()
-        piece(0, PIECES - 1, mid).start()
-        for c in range(1, chunks):
-            own_features[c].wait()
-            from_end(c, mid).start()
-        for copy in small[2:]:
+        for copy in small:
             copy.wait()
         pack_tower()
         far_tower(d, far).start()
-        each(fields // 2, lambda k: end_weight(1, k).wait())
+        for copy in own_features:
+            copy.wait()
+        from_end(0, mid).start()
+        piece(0, PIECES - 1, mid).start()
+        from_end(1, mid).start()
+        bias_copy(mid).start()
+        for c in range(2, chunks):
+            from_end(c, mid).start()
+        loaded_end(1)
         for p in range(PIECES):
             piece(1, p, mid).start()
         near_tower(mid).start()
+        unit_sends()
 
     def expect_piece(level, p):
         piece(level, p, end).wait_recv()
@@ -727,11 +747,11 @@
     def expect_end(c):
         from_end(c, end).wait_recv()
         cross(1, c, end).start()
-        pair(c, end, f).start()
+        pair(c, end).start()
 
     def expect_far(k, c, o):
         cross(k, c, o).wait_recv()
-        pair(c, o, f).start()
+        pair(c, o).start()
 
     def expect_tower(i, z):
         far_tower(z, end).wait_recv()
@@ -775,21 +795,21 @@
 
         @pl.when(c == 2)
         def _():
+            expect_far(1, 2, far_end)
             plane_forward(FAR_TOWER)
-            expect_far(1, 2, far_end)
+            plane_forward(END_TOWER)
+            expect_piece(1, 0)
 
         @pl.when(c == 3)
         def _():
-            expect_tower(END_TOWER, far_end)
             expect_far(1, 3, far_end)
-            expect_piece(1, 0)
+            expect_piece(1, 1)
 
         def wait_pair():
-            for o in range(dim_count):
-                pair(c, o, other).wait_recv()
+            landed(x0.at[c, fs], pair_recv.at[c])
 
         x1[c, fs, ss, :] = advance(x0, 0, c, wait_pair)
-        pair_one(c, side, f).start()
+        pair_one(c, side).start()
 
         @pl.when(c > 0)
         def _():
@@ -801,13 +821,13 @@
         matrix = tw[:, :, :side_k].reshape(members * units, side_k)
         return jnp.dot(matrix, x2[c].reshape(side_k, lanes), preferred_element_type=jnp.float32)
 
+    def expect_one(c):
+        cross_one(c, 1 - side).wait_recv()
+        pair_one(c, 1 - side).start()
+
     def layer_two(c):
-        cross_one(c, 1 - side).wait_recv()
-        pair_one(c, 1 - side, f).start()
-
         def wait_pair():
-            pair_one(c, side, other).wait_recv()
-            pair_one(c, 1 - side, other).wait_recv()
+            landed(x1.at[c, fs], one_recv.at[c])
 
         y[c] = advance(x1, 1, c, wait_pair)
         two(c, f).start()
@@ -832,17 +852,24 @@
             part(c).start()
 
     def second(c, carry):
-        @pl.when(c < chunks)
+        layer_two(c)
+
+        @pl.when(c == 1)
         def _():
-            layer_two(c)
-
-        @pl.when(c > 0)
+            expect_one(2)
+
+        def tower_step(k, carry):
+            layer_three(k)
+            return carry
+
+        last = c == chunks - 1
+        lax.fori_loop(
+            jnp.where(last, c, jnp.maximum(c - 1, 0)), jnp.where(c < chunks - 2, c, c + 1),
+            tower_step, 0)
+
+        @pl.when(c == 2)
         def _():
-            layer_three(c - 1)
-
-        @pl.when(owner & (c > 1))
-        def _():
-            finish(c - 2)
+            expect_one(3)
 
         return carry
 
@@ -863,146 +890,123 @@
         picked = jnp.sum(jnp.where(labels == target, logits, 0.0), axis=0, keepdims=True)
         best = jnp.max(logits, axis=0, keepdims=True)
         total = jnp.sum(jnp.exp(logits - best), axis=0, keepdims=True)
-        losses[c, f] = best + jnp.log(total) - picked
+        losses[f, c] = best + jnp.log(total) - picked
         for k in range(1, members):
-            loss_copy(k, c, f).start()
+            loss_copy(k, c).start()
 
     @pl.when(is_mid)
     def _():
         for c in range(chunks):
             own_features[c].wait()
             cross(0, c, mid).start()
-            pair(c, mid, f).start()
-        small[1].wait()
-        unit_sends(lambda copy: copy.start())
-        for copy in small[:1] + small[2:]:
+            pair(c, mid).start()
+        for copy in small:
             copy.wait()
         for k in range(1, batch_count):
-            cand_copy(k, b).start()
+            cand_copy(k).start()
         pack_tower()
         far_tower(d, far).start()
         tw[me] = tw_near[...]
         both(mid, f).start()
-        bias_copy(end).wait_recv()
-        build_bias()
         expect_piece(0, 0)
         expect_far(0, 0, far)
         expect_piece(0, 1)
         expect_far(0, 1, far)
-        plane_forward(0)
         expect_piece(0, 2)
         expect_far(0, 2, far)
+        plane_forward(0)
         plane_forward(1)
+        expect_far(0, 3, far)
         expect_end(0)
-        expect_far(0, 3, far)
+        expect_piece(0, 3)
         plane_forward(2)
-        expect_tower(FAR_TOWER, far)
-        expect_piece(0, 3)
         expect_far(1, 0, far_end)
         expect_end(1)
         plane_forward(3)
+        expect_tower(FAR_TOWER, far)
+        expect_tower(END_TOWER, far_end)
+        bias_copy(end).wait_recv()
+        build_bias()
+        unit_sends()
         for level in range(CROSS):
-            each(fields, lambda k: own_weight(level, k).wait())
+            loaded_own(level)
         expect_end(2)
-        for p in range(PIECES):
-            plane_rest(p)
+        plane_rest(0)
         expect_far(1, 1, far_end)
         lax.fori_loop(0, chunks, first, 0)
-        plane_forward(END_TOWER)
-        for k in range(1, batch_count):
-            cand_copy(0, lax.rem(b + k, batch_count)).wait_recv()
-        for m in range(members):
-            @pl.when(me != m)
-            def _():
-                unit_copy(0, m, f, d).wait_recv()
-        build_units()
-        expect_piece(1, 1)
+        landed(cands.at[pl.ds(0, batch_count - 1)], cand_recv)
+        plane_rest(2)
+        both(far, f).start()
+        both(far_end, f).start()
+        expect_piece(1, 2)
+        expect_piece(1, 3)
         plane_forward(PIECES)
-        expect_piece(1, 2)
         plane_forward(PIECES + 1)
-        expect_piece(1, 3)
-        for i, z in ((FAR_TOWER, far), (END_TOWER, far_end)):
-            plane_rest(i)
-            both(z, f).start()
+        expect_one(0)
         plane_forward(PIECES + 2)
         plane_forward(PIECES + 3)
+        expect_one(1)
         near_tower(end).wait_recv()
         both(end, f).start()
-        for p in range(PIECES):
-            plane_rest(PIECES + p)
-        for z in range(dim_count):
-            both(z, other).wait_recv()
-        lax.fori_loop(0, chunks + 1, second, 0)
+        landed(unit_raw.at[pl.ds(0, members - 1)], unit_recv)
+        build_units()
+        plane_rest(1)
+        landed(tw.at[pl.ds(0, dim_count)], both_recv)
+        lax.fori_loop(0, chunks, second, 0)
 
         @pl.when(owner)
         def _():
-            finish(chunks - 1)
-
-    for c in range(chunks):
-        for ff in range(field_count):
-            @pl.when(jnp.logical_not((d == 1 + ff) & (f == ff)))
-            def _():
-                loss_copy(1, c, ff).wait_recv()
-
-    for c in range(chunks):
-        for ff in range(field_count):
-            loss_out[c * field_count + ff] = losses[c, ff]
+            for c in range(chunks):
+                finish(c)
+
+    @pl.when(owner)
+    def _():
+        landed(losses.at[0], loss_recv)
+
+    @pl.when(jnp.logical_not(owner))
+    def _():
+        landed(losses, loss_recv)
+
+    for ff in range(field_count):
+        for c in range(chunks):
+            loss_out[c * field_count + ff] = losses[ff, c]
 
     @pl.when(is_end)
     def _():
         for level in range(CROSS):
-            for p in range(PIECES):
-                piece(level, p, mid).wait_send()
-        for c in range(chunks):
-            from_end(c, mid).wait_send()
-            give(c).wait_recv()
+            sent(weight_part(level, 0, fl, b), piece_send.at[level])
+        sent(x0.at[:, fs, entries(d), :], end_send)
         bias_copy(mid).wait_send()
         near_tower(mid).wait_send()
         far_tower(d, far).wait_send()
-
-    unit_sends(lambda copy: copy.wait_send())
+        sent(unit_raw.at[pl.ds(0, 4)], unit_send)
+        landed(out, give_recv)
 
     @pl.when(is_mid)
     def _():
         far_tower(d, far).wait_send()
-        for k in range(1, batch_count):
-            cand_copy(k, b).wait_send()
-        for z in range(dim_count):
-            both(z, f).wait_send()
-
-        def drain(c, carry):
-            cross(0, c, mid).wait_send()
-            cross(1, c, end).wait_send()
-            cross_one(c, side).wait_send()
-            for o in range(dim_count):
-                pair(c, o, f).wait_send()
-            for s in range(2):
-                pair_one(c, s, f).wait_send()
-            two(c, f).wait_send()
-            give(c).wait_send()
-            keep(c).wait()
-            return carry
-
-        lax.fori_loop(0, chunks, drain, 0)
-
-        for i in range(END_TOWER + 1):
-            plane(i, 0, b, x_next).wait_send()
-            plane(i, 1, b, y_next).wait_send()
-            plane(i, 2, *relay(i)).wait_send()
+        sent(cands.at[pl.ds(0, batch_count - 1)], cand_send)
+        sent(tw.at[pl.ds(0, dim_count)], both_send)
+        sent(unit_raw.at[pl.ds(0, 3)], unit_send)
+        sent(x0.at[:, fs, entries(mid), :], cross_send.at[0])
+        sent(x0.at[:, fs, entries(end), :], cross_send.at[1])
+        sent(x1.at[:, fs, ss, :], cross_send.at[2])
+        sent(x0.at[:, fs], pair_send)
+        sent(x1.at[:, fs], one_send)
+        sent(y.at[:, :, :, pl.ds(0, lanes)], two_send)
+        sent(out, give_send)
+        pltpu.make_async_copy(out, out, out_sem).wait()
+        for group in range(CROSS + 1):
+            sent(plane_bytes(group, 3), plane_send.at[group])
 
     @pl.when(giver)
     def _():
-        for c in range(chunks):
-            part(c).wait_send()
+        sent(pre_out, part_send)
 
     @pl.when(owner)
     def _():
-        def drain_losses(c, carry):
-            for k in range(1, members):
-                loss_copy(k, c, f).wait_send()
-            return carry
-
-        lax.fori_loop(0, chunks, drain_losses, 0)
+        for k in range(1, members):
+            sent(losses.at[0], loss_send.at[k])
 
 
 def line_body(
@@ -1054,15 +1058,14 @@
             vmem((batch_count,) + candidates.shape, bf16),
             vmem(user_vec.shape, bf16),
             vmem((CHUNKS * field_count, 1, lanes), jnp.int32),
-            vmem((CHUNKS, field_count, 1, lanes), f32),
-            dma((CHUNKS,)), dma((CROSS, fields)), dma((7,)),
-            dma((CHUNKS,)), dma((CHUNKS,)), dma((3, CHUNKS)), dma((3, CHUNKS)),
-            dma((dim_count, CHUNKS)), dma((dim_count, CHUNKS)), dma((2, CHUNKS)), dma((2, CHUNKS)),
-            dma((CROSS, PIECES)), dma((CROSS, PIECES)), dma((items, 3)), dma((items, batch_count)),
-            dma((2,)), dma((dim_count,)), dma((dim_count,)), dma((dim_count,)),
-            dma, dma, dma((members,)), dma((members,)), dma((batch_count,)), dma((batch_count,)),
-            dma((CHUNKS,)), dma((CHUNKS,)), dma((CHUNKS,)), dma((CHUNKS,)), dma((CHUNKS,)),
-            dma((CHUNKS,)), dma((CHUNKS,)), dma((CHUNKS, members)), dma((CHUNKS, field_count)),
+            vmem((field_count, CHUNKS, 1, lanes), f32),
+            dma((CHUNKS,)), dma((CROSS,)), dma((7,)),
+            dma, dma((CHUNKS,)), dma((3,)), dma((3, CHUNKS)),
+            dma, dma((CHUNKS,)), dma, dma((CHUNKS,)),
+            dma((CROSS,)), dma((CROSS, PIECES)), dma((CROSS + 1,)), dma((items,)), dma((CROSS + 1,)),
+            dma((2,)), dma((dim_count,)), dma, dma,
+            dma, dma, dma, dma, dma, dma,
+            dma, dma((CHUNKS,)), dma, dma, dma, dma, dma((CHUNKS,)), dma((members,)), dma,
         ],
         compiler_params=pltpu.CompilerParams(
             collective_id=0, has_side_effects=True, vmem_limit_bytes=60 * 2**20),

time: 118 us -> 108 us (0.915)
  Pallas kernels: 114 us -> 104 us
    pallas_call x1, Pallas kernels: 114 us -> 104 us  [line_body(): pl.pallas_call(functools.partial(line_kernel, counts), out_shape=(jax.Sha...]
where the time goes in v3:
time: 108 us
  Pallas kernels  104 us (96%)
  local copies, waits for them, and re-layouts  3.39 us (3%)
    pallas_call x1, Pallas kernels, line_body(): pl.pallas_call(functools.partial(line_kernel, counts), out_shape=(jax.Sha...  104 us
    unnamed x2, local copies, waits for them, and re-layouts  3.39 us

profile of v3, /device:TPU:0, one launch (start us, length us, event | category | flops | bytes accessed | tf_op | source)
XLA Modules:
  0.0 107.7 jit_solution(11304794995504835141)
XLA Ops:
  0.6 103.6 %line_forward.1 = (bf16[13,32,1024]{2,1,0:T(8,128)(2,1)}, f32[8,1,128]{2,1,0:T(1,128)}) custom-call(bf16[13,32,1024]{2,1,0:T(8,128)(2,1)} %feat.1, bf16[2,13,26,32,128]{4,3,2,1,0:T(8,128)(2,1)} %bitcast.6, f32[13,2,32]{2,1,0:T(2,128)} %bitcast.8, bf16[26,128,128]{2,1,0:T(8,128)(2,1)} %bitcast.7, f32[1,128]{1,0:T(1,128)} %bitcast.11, ...), custom_call_target="tpu_custom_call" | custom-call | tf_op jit(solution)/shard_map/line_forward/pallas_call | solution.py:1032
  104.3 2.1 %copy.13 = bf16[13,32,1024]{2,1,0:T(8,128)(2,1)} copy(bf16[13,32,1024]{2,1,0:T(8,128)(2,1)} %get-tuple-element.8) | data formatting | bytes 1703936
  106.4 1.3 %copy.14 = f32[1024]{0:T(1024)} copy(f32[1024]{0:T(1024)} %bitcast.10) | data formatting | bytes 8192

commit v4 on v3

--- a/solution.py
+++ b/solution.py
@@ -618,8 +618,11 @@
     def loss_copy(k, c):
         m = lax.rem(me + k, members)
         return remote(
-            losses.at[f, c], loss_send.at[k], loss_recv,
+            losses.at[c], loss_send.at[k], loss_recv, to=loss_out.at[c * field_count + f],
             field=m // dim_count, dim=lax.rem(m, dim_count))
+
+    def keep_loss(c):
+        return pltpu.make_async_copy(losses.at[c], loss_out.at[c * field_count + f], loss_send.at[0])
 
     def own_weight(level, ff):
         return pltpu.make_async_copy(
@@ -656,25 +659,6 @@
         pltpu.make_async_copy(user, users, small_sem.at[5]),
         pltpu.make_async_copy(positive, targets, small_sem.at[6]),
     ]
-    for copy in own_features:
-        copy.start()
-
-    @pl.when(is_end)
-    def _():
-        each(fields // 2, lambda k: end_weight(0, k).start())
-
-    for copy in small:
-        copy.start()
-
-    @pl.when(is_mid)
-    def _():
-        each(fields, lambda k: own_weight(0, k).start())
-        each(fields, lambda k: own_weight(1, k).start())
-
-    @pl.when(is_end)
-    def _():
-        each(fields // 2, lambda k: end_weight(1, k).start())
-
     barrier = pltpu.get_barrier_semaphore()
     for k in range(1, members):
         m = lax.rem(me + k, members)
@@ -684,6 +668,25 @@
     for k in range(1, batch_count):
         pl.semaphore_signal(
             barrier, inc=1, device_id={"batch": lax.rem(b + k, batch_count)}, device_id_type=MESH)
+    for copy in own_features:
+        copy.start()
+
+    @pl.when(is_end)
+    def _():
+        each(fields // 2, lambda k: end_weight(0, k).start())
+
+    for copy in small:
+        copy.start()
+
+    @pl.when(is_mid)
+    def _():
+        each(fields, lambda k: own_weight(0, k).start())
+        each(fields, lambda k: own_weight(1, k).start())
+
+    @pl.when(is_end)
+    def _():
+        each(fields // 2, lambda k: end_weight(1, k).start())
+
     pl.semaphore_wait(barrier, members + batch_count - 2)
 
     def unit_sends():
@@ -890,9 +893,10 @@
         picked = jnp.sum(jnp.where(labels == target, logits, 0.0), axis=0, keepdims=True)
         best = jnp.max(logits, axis=0, keepdims=True)
         total = jnp.sum(jnp.exp(logits - best), axis=0, keepdims=True)
-        losses[f, c] = best + jnp.log(total) - picked
+        losses[c] = best + jnp.log(total) - picked
         for k in range(1, members):
             loss_copy(k, c).start()
+        keep_loss(c).start()
 
     @pl.when(is_mid)
     def _():
@@ -961,15 +965,11 @@
 
     @pl.when(owner)
     def _():
-        landed(losses.at[0], loss_recv)
+        landed(losses, loss_recv)
 
     @pl.when(jnp.logical_not(owner))
     def _():
-        landed(losses, loss_recv)
-
-    for ff in range(field_count):
-        for c in range(chunks):
-            loss_out[c * field_count + ff] = losses[ff, c]
+        landed(loss_out, loss_recv)
 
     @pl.when(is_end)
     def _():
@@ -1006,7 +1006,8 @@
     @pl.when(owner)
     def _():
         for k in range(1, members):
-            sent(losses.at[0], loss_send.at[k])
+            sent(losses, loss_send.at[k])
+        pltpu.make_async_copy(losses, losses, loss_send.at[0]).wait()
 
 
 def line_body(
@@ -1028,7 +1029,6 @@
     bf16 = jnp.bfloat16
     f32 = jnp.float32
     far = pl.BlockSpec(memory_space=pl.ANY)
-    near = pl.BlockSpec(memory_space=pltpu.VMEM)
     crossed, losses = pl.pallas_call(
         functools.partial(line_kernel, counts),
         out_shape=(
@@ -1036,7 +1036,7 @@
             jax.ShapeDtypeStruct((CHUNKS * field_count, 1, lanes), f32),
         ),
         in_specs=[far] * 9,
-        out_specs=(far, near),
+        out_specs=(far, far),
         scratch_shapes=[
             vmem((CHUNKS, fields, width, rc), bf16),
             vmem((CHUNKS, fields, width, rc), bf16),
@@ -1058,7 +1058,7 @@
             vmem((batch_count,) + candidates.shape, bf16),
             vmem(user_vec.shape, bf16),
             vmem((CHUNKS * field_count, 1, lanes), jnp.int32),
-            vmem((field_count, CHUNKS, 1, lanes), f32),
+            vmem((CHUNKS, 1, lanes), f32),
             dma((CHUNKS,)), dma((CROSS,)), dma((7,)),
             dma, dma((CHUNKS,)), dma((3,)), dma((3, CHUNKS)),
             dma, dma((CHUNKS,)), dma, dma((CHUNKS,)),
@@ -1068,9 +1068,9 @@
             dma, dma((CHUNKS,)), dma, dma, dma, dma, dma((CHUNKS,)), dma((members,)), dma,
         ],
         compiler_params=pltpu.CompilerParams(
-            collective_id=0, has_side_effects=True, vmem_limit_bytes=60 * 2**20),
+            collective_id=0, has_side_effects=True, vmem_limit_bytes=48 * 2**20),
         name="line_forward",
-    )(
+    )(*(pltpu.with_memory_space_constraint(value, pltpu.HBM) for value in (
         features,
         cross_weight.transpose(0, 1, 3, 2, 4),
         cross_bias.transpose(1, 0, 2),
@@ -1080,7 +1080,7 @@
         user_vec,
         candidates,
         positive.reshape(CHUNKS * field_count, 1, lanes),
-    )
+    )))
     return (crossed, losses.reshape(row_count))
 
 

time: 108 us -> 105 us (0.972)
  Pallas kernels: 104 us -> 102 us
  local copies, waits for them, and re-layouts: 3.39 us -> 1.5 us
    unnamed x2, local copies, waits for them, and re-layouts: 3.39 us -> 1.5 us
    pallas_call x1, Pallas kernels: 104 us -> 102 us  [line_body(): pl.pallas_call(functools.partial(line_kernel, counts), out_shape=(jax.Sha...]
where the time goes in v4:
time: 105 us
  Pallas kernels  102 us (97%)
  local copies, waits for them, and re-layouts  1.5 us (1%)
    pallas_call x1, Pallas kernels, line_body(): pl.pallas_call(functools.partial(line_kernel, counts), out_shape=(jax.Sha...  102 us

profile of v4, /device:TPU:0, one launch (start us, length us, event | category | flops | bytes accessed | tf_op | source)
XLA Modules:
  0.0 104.6 jit_solution(13176555876594455211)
XLA Ops:
  0.6 102.4 %line_forward.1 = (bf16[13,32,1024]{2,1,0:T(8,128)(2,1)S(1)}, f32[8,1,128]{2,1,0:T(1,128)S(1)}) custom-call(bf16[13,32,1024]{2,1,0:T(8,128)(2,1)} %feat.1, bf16[2,13,26,32,128]{4,3,2,1,0:T(8,128)(2,1)} %bitcast.7, f32[13,2,32]{2,1,0:T(2,128)} %bitcast.9, bf16[26,128,128]{2,1,0:T(8,128)(2,1)} %bitcast.8, f32[1,128]{1,0:T(1,128)} %bitcast.11, ...), custom_call_target="tpu_custom_call" | custom-call | tf_op jit(solution)/shard_map/line_forward/pallas_call | solution.py:1032
  103.1 0.9 copy.13
  104.0 0.6 copy.14

commit v5 on v4

--- a/solution.py
+++ b/solution.py
@@ -446,19 +446,20 @@
 CHUNKS = 4
 FAR_TOWER = CROSS * PIECES
 END_TOWER = FAR_TOWER + 1
+CANDS = END_TOWER + 1
 
 
 def line_kernel(
     counts,
     feat, weight, bias, tower, tower_bias, query_weight, user, cand, positive,
     out, loss_out,
-    x0, x1, y, x2, flat, tw, tw_near, tw_far, tw_raw, q_raw, pre_out, pre_in, pre_own,
+    x0, x1, y, x2, flat, tw, tw_near, tw_far, tw_pass, tw_raw, q_raw, pre_out, pre_in, pre_own,
     bias_raw, bias_cols, unit_raw, unit_cols, cands, users, targets, losses,
     feat_sem, weight_sem, small_sem,
     end_send, end_recv, cross_send, cross_recv, pair_send, pair_recv, one_send, one_recv,
     piece_send, piece_recv, plane_send, plane_recv, rest_recv,
-    tower_send, tower_recv, both_send, both_recv,
-    bias_send, bias_recv, unit_send, unit_recv, cand_send, cand_recv,
+    tower_send, tower_recv, near_recv, both_send, both_recv,
+    bias_send, bias_recv, unit_send, unit_recv, near_unit,
     two_send, two_recv, out_sem, give_send, give_recv, part_send, part_recv, loss_send, loss_recv,
 ):
     batch_count, field_count, dim_count = counts
@@ -547,24 +548,28 @@
     def item(i, source):
         if i < CROSS * PIECES:
             return weight_piece(i // PIECES, i % PIECES, source)
+        if i == CANDS:
+            return cands.at[source]
         return tower_rows(f * dim_count + (far if i == FAR_TOWER else far_end), source)
 
     def relay(i):
         return (x_next, y_next) if i % 2 == 0 else (y_next, x_next)
 
+    def group_of(i):
+        return CROSS + 1 if i == CANDS else i // PIECES
+
     def plane(i, source, target, arrival):
-        group = i // PIECES
-        return remote(item(i, source), plane_send.at[group], arrival, batch=target)
+        return remote(item(i, source), plane_send.at[group_of(i)], arrival, batch=target)
 
     def plane_out(i):
         first, second = relay(i)
         plane(i, b, first, plane_recv.at[i]).start()
-        plane(i, b, second, rest_recv.at[i // PIECES]).start()
+        plane(i, b, second, rest_recv.at[group_of(i)]).start()
 
     def plane_forward(i):
         source, target = relay(i)
         plane(i, source, target, plane_recv.at[i]).wait_recv()
-        plane(i, source, target, rest_recv.at[i // PIECES]).start()
+        plane(i, source, target, rest_recv.at[group_of(i)]).start()
 
     def plane_rest(group):
         landed(plane_bytes(group, 2), rest_recv.at[group])
@@ -572,28 +577,39 @@
     def plane_bytes(group, copies):
         if group < CROSS:
             return flat.at[group, :, pl.ds(0, copies * rows_in_part), pl.ds(0, half_k)]
+        if group == CROSS + 1:
+            return cands.at[pl.ds(0, copies)]
         return tw.at[pl.ds(0, copies * 2), pl.ds(0, quarter_units), :]
 
     def near_tower(target):
         return remote(
-            tw_near, tower_send.at[0], tower_recv.at[end], to=tw.at[f * dim_count + end], dim=target)
+            tw_near, tower_send.at[0], near_recv, to=tw.at[f * dim_count + end], dim=target)
 
     def far_tower(source, target):
         return remote(
             tw_far, tower_send.at[1], tower_recv.at[source],
             to=tower_rows(f * dim_count + source, b), dim=target)
 
+    def pass_in(target):
+        return remote(tw_far, tower_send.at[1], tower_recv.at[mid], to=tw_pass, dim=target)
+
+    def pass_on():
+        return remote(
+            tw_pass, tower_send.at[0], tower_recv.at[end],
+            to=tower_rows(f * dim_count + end, b), dim=far)
+
     def both(z, ff):
         return remote(tw.at[ff * dim_count + z], both_send, both_recv, field=other)
 
     def bias_copy(target):
         return remote(bias_raw.at[lax.rem(end, 2)], bias_send, bias_recv, dim=target)
 
-    def unit_copy(ff, z):
-        return remote(unit_raw.at[me], unit_send, unit_recv, field=ff, dim=z)
-
-    def cand_copy(k):
-        return remote(cands.at[b], cand_send, cand_recv, batch=lax.rem(b + k, batch_count))
+    def unit_in(target):
+        return remote(unit_raw.at[f * dim_count + end], unit_send, near_unit, dim=target)
+
+    def unit_out(ff, z):
+        rows = unit_raw.at[pl.ds(f * dim_count + 2 * side, 2)]
+        return remote(rows, unit_send, unit_recv, field=ff, dim=z)
 
     def two(c, ff):
         lane = pl.multiple_of((1 - ff) * lanes, lanes)
@@ -660,14 +676,25 @@
         pltpu.make_async_copy(positive, targets, small_sem.at[6]),
     ]
     barrier = pltpu.get_barrier_semaphore()
-    for k in range(1, members):
-        m = lax.rem(me + k, members)
-        pl.semaphore_signal(
-            barrier, inc=1, device_id={"field": m // dim_count, "dim": lax.rem(m, dim_count)},
-            device_id_type=MESH)
-    for k in range(1, batch_count):
-        pl.semaphore_signal(
-            barrier, inc=1, device_id={"batch": lax.rem(b + k, batch_count)}, device_id_type=MESH)
+
+    def greet(**where):
+        pl.semaphore_signal(barrier, inc=1, device_id=where, device_id_type=MESH)
+
+    @pl.when(is_end)
+    def _():
+        for ff in range(field_count):
+            for z in (1, 2):
+                greet(field=ff, dim=z)
+
+    @pl.when(is_mid)
+    def _():
+        greet(dim=end)
+        greet(dim=far)
+        greet(batch=x_next)
+        greet(batch=y_next)
+        greet(field=other, dim=far)
+        greet(field=other)
+
     for copy in own_features:
         copy.start()
 
@@ -687,14 +714,7 @@
     def _():
         each(fields // 2, lambda k: end_weight(1, k).start())
 
-    pl.semaphore_wait(barrier, members + batch_count - 2)
-
-    def unit_sends():
-        for ff in range(field_count):
-            for z in (1, 2):
-                @pl.when((f != ff) | (d != z))
-                def _():
-                    unit_copy(ff, z).start()
+    pl.semaphore_wait(barrier, jnp.where(is_mid, 2 * field_count + 5, 1))
 
     def loaded_own(level):
         ref = flat.at[level, :, within(mid), :]
@@ -728,20 +748,20 @@
         for copy in small:
             copy.wait()
         pack_tower()
-        far_tower(d, far).start()
+        pass_in(mid).start()
         for copy in own_features:
             copy.wait()
         from_end(0, mid).start()
         piece(0, PIECES - 1, mid).start()
         from_end(1, mid).start()
         bias_copy(mid).start()
+        unit_in(mid).start()
         for c in range(2, chunks):
             from_end(c, mid).start()
         loaded_end(1)
         for p in range(PIECES):
             piece(1, p, mid).start()
         near_tower(mid).start()
-        unit_sends()
 
     def expect_piece(level, p):
         piece(level, p, end).wait_recv()
@@ -791,11 +811,6 @@
             unit_cols[m * units:(m + 1) * units, :] = jnp.broadcast_to(unit_raw[m], (lanes, units)).T
 
     def first(c, carry):
-        @pl.when(c == 1)
-        def _():
-            expect_end(3)
-            cross_one(0, side).start()
-
         @pl.when(c == 2)
         def _():
             expect_far(1, 2, far_end)
@@ -812,12 +827,8 @@
             landed(x0.at[c, fs], pair_recv.at[c])
 
         x1[c, fs, ss, :] = advance(x0, 0, c, wait_pair)
+        cross_one(c, side).start()
         pair_one(c, side).start()
-
-        @pl.when(c > 0)
-        def _():
-            cross_one(c, side).start()
-
         return carry
 
     def tower_part(c):
@@ -906,8 +917,7 @@
             pair(c, mid).start()
         for copy in small:
             copy.wait()
-        for k in range(1, batch_count):
-            cand_copy(k).start()
+        plane_out(CANDS)
         pack_tower()
         far_tower(d, far).start()
         tw[me] = tw_near[...]
@@ -916,7 +926,10 @@
         expect_far(0, 0, far)
         expect_piece(0, 1)
         expect_far(0, 1, far)
+        plane_forward(CANDS)
         expect_piece(0, 2)
+        pass_in(end).wait_recv()
+        pass_on().start()
         expect_far(0, 2, far)
         plane_forward(0)
         plane_forward(1)
@@ -924,21 +937,25 @@
         expect_end(0)
         expect_piece(0, 3)
         plane_forward(2)
-        expect_far(1, 0, far_end)
         expect_end(1)
         plane_forward(3)
+        expect_far(1, 0, far_end)
         expect_tower(FAR_TOWER, far)
         expect_tower(END_TOWER, far_end)
         bias_copy(end).wait_recv()
         build_bias()
-        unit_sends()
+        unit_in(end).wait_recv()
+        unit_out(other, d).start()
+        unit_out(f, far).start()
+        unit_out(other, far).start()
         for level in range(CROSS):
             loaded_own(level)
         expect_end(2)
         plane_rest(0)
         expect_far(1, 1, far_end)
+        expect_end(3)
         lax.fori_loop(0, chunks, first, 0)
-        landed(cands.at[pl.ds(0, batch_count - 1)], cand_recv)
+        plane_rest(3)
         plane_rest(2)
         both(far, f).start()
         both(far_end, f).start()
@@ -952,7 +969,7 @@
         expect_one(1)
         near_tower(end).wait_recv()
         both(end, f).start()
-        landed(unit_raw.at[pl.ds(0, members - 1)], unit_recv)
+        landed(unit_raw.at[pl.ds(0, 6)], unit_recv)
         build_units()
         plane_rest(1)
         landed(tw.at[pl.ds(0, dim_count)], both_recv)
@@ -978,16 +995,16 @@
         sent(x0.at[:, fs, entries(d), :], end_send)
         bias_copy(mid).wait_send()
         near_tower(mid).wait_send()
+        pass_in(mid).wait_send()
+        unit_in(mid).wait_send()
+        landed(out, give_recv)
+
+    @pl.when(is_mid)
+    def _():
         far_tower(d, far).wait_send()
-        sent(unit_raw.at[pl.ds(0, 4)], unit_send)
-        landed(out, give_recv)
-
-    @pl.when(is_mid)
-    def _():
-        far_tower(d, far).wait_send()
-        sent(cands.at[pl.ds(0, batch_count - 1)], cand_send)
+        pass_on().wait_send()
         sent(tw.at[pl.ds(0, dim_count)], both_send)
-        sent(unit_raw.at[pl.ds(0, 3)], unit_send)
+        sent(unit_raw.at[pl.ds(0, 6)], unit_send)
         sent(x0.at[:, fs, entries(mid), :], cross_send.at[0])
         sent(x0.at[:, fs, entries(end), :], cross_send.at[1])
         sent(x1.at[:, fs, ss, :], cross_send.at[2])
@@ -996,7 +1013,7 @@
         sent(y.at[:, :, :, pl.ds(0, lanes)], two_send)
         sent(out, give_send)
         pltpu.make_async_copy(out, out, out_sem).wait()
-        for group in range(CROSS + 1):
+        for group in range(CROSS + 2):
             sent(plane_bytes(group, 3), plane_send.at[group])
 
     @pl.when(giver)
@@ -1023,7 +1040,7 @@
     wide = 2 * el
     quarter = units // batch_count
     packed = fields * wide + width
-    items = END_TOWER + 1
+    items = CANDS + 1
     dma = pltpu.SemaphoreType.DMA
     vmem = pltpu.VMEM
     bf16 = jnp.bfloat16
@@ -1046,6 +1063,7 @@
             vmem((members, units, packed), bf16),
             vmem((units, packed), bf16),
             vmem((quarter, packed), bf16),
+            vmem((quarter, packed), bf16),
             vmem((fields, units, width), bf16),
             vmem((units, width), bf16),
             vmem((CHUNKS, members * units, lanes), bf16),
@@ -1062,9 +1080,9 @@
             dma((CHUNKS,)), dma((CROSS,)), dma((7,)),
             dma, dma((CHUNKS,)), dma((3,)), dma((3, CHUNKS)),
             dma, dma((CHUNKS,)), dma, dma((CHUNKS,)),
-            dma((CROSS,)), dma((CROSS, PIECES)), dma((CROSS + 1,)), dma((items,)), dma((CROSS + 1,)),
-            dma((2,)), dma((dim_count,)), dma, dma,
-            dma, dma, dma, dma, dma, dma,
+            dma((CROSS,)), dma((CROSS, PIECES)), dma((CROSS + 2,)), dma((items,)), dma((CROSS + 2,)),
+            dma((2,)), dma((dim_count,)), dma, dma, dma,
+            dma, dma, dma, dma, dma,
             dma, dma((CHUNKS,)), dma, dma, dma, dma, dma((CHUNKS,)), dma((members,)), dma,
         ],
         compiler_params=pltpu.CompilerParams(

time: 105 us -> 103 us (0.981)
  Pallas kernels: 102 us -> 100 us
    pallas_call x1, Pallas kernels: 102 us -> 100 us  [line_body(): pl.pallas_call(functools.partial(line_kernel, counts), out_shape=(jax.Sha...]
where the time goes in v5:
time: 103 us
  Pallas kernels  100 us (97%)
  local copies, waits for them, and re-layouts  1.5 us (1%)
    pallas_call x1, Pallas kernels, line_body(): pl.pallas_call(functools.partial(line_kernel, counts), out_shape=(jax.Sha...  100 us

profile of v5, /device:TPU:0, one launch (start us, length us, event | category | flops | bytes accessed | tf_op | source)
XLA Modules:
  0.0 102.5 jit_solution(2519404604606384262)
XLA Ops:
  0.6 100.4 %line_forward.1 = (bf16[13,32,1024]{2,1,0:T(8,128)(2,1)S(1)}, f32[8,1,128]{2,1,0:T(1,128)S(1)}) custom-call(bf16[13,32,1024]{2,1,0:T(8,128)(2,1)} %feat.1, bf16[2,13,26,32,128]{4,3,2,1,0:T(8,128)(2,1)} %bitcast.7, f32[13,2,32]{2,1,0:T(2,128)} %bitcast.9, bf16[26,128,128]{2,1,0:T(8,128)(2,1)} %bitcast.8, f32[1,128]{1,0:T(1,128)} %bitcast.11, ...), custom_call_target="tpu_custom_call" | custom-call | tf_op jit(solution)/shard_map/line_forward/pallas_call | solution.py:1049
  101.0 0.9 copy.13
  101.9 0.6 copy.14

commit v6 on v5

--- a/solution.py
+++ b/solution.py
@@ -436,13 +436,16 @@
     batch_count, field_count, dim_count = counts
     fl, el, row_count = features.shape
     units, fields, width = tower_weight.shape
+    relayed = line_pieces(fl, PIECES)[RELAYED][0]
     return (
+        (fl + relayed) % 2 == 0 and (2 * fl + relayed) % 3 == 0 and
         dim_count == 4 and batch_count == 4 and field_count == 2
         and fields % 2 == 0 and fl >= PIECES and el % 32 == 0 and 4 * el == width and width == 128
         and row_count % (CHUNKS * field_count * 128) == 0 and units % (16 * batch_count) == 0)
 
 
 PIECES = 4
+RELAYED = 2
 CHUNKS = 4
 FAR_TOWER = CROSS * PIECES
 END_TOWER = FAR_TOWER + 1
@@ -457,7 +460,7 @@
     bias_raw, bias_cols, unit_raw, unit_cols, cands, users, targets, losses,
     feat_sem, weight_sem, small_sem,
     end_send, end_recv, cross_send, cross_recv, pair_send, pair_recv, one_send, one_recv,
-    piece_send, piece_recv, plane_send, plane_recv, rest_recv,
+    piece_send, piece_recv, direct_load, direct_send, direct_recv, plane_send, plane_recv, rest_recv,
     tower_send, tower_recv, near_recv, both_send, both_recv,
     bias_send, bias_recv, unit_send, unit_recv, near_unit,
     two_send, two_recv, out_sem, give_send, give_recv, part_send, part_recv, loss_send, loss_recv,
@@ -484,8 +487,9 @@
     far_end = 3 - end
     is_mid = d == mid
     is_end = d == end
-    owner = is_mid & (f == side)
-    giver = is_mid & (f != side)
+    owner = is_mid & (f == 1)
+    giver = is_mid & (f == 0)
+    part_of = jnp.where(f == 1, side, 1 - side)
     other = field_count - 1 - f
     x_next = b + 1 - 2 * lax.rem(b, 2)
     y_next = lax.rem(b + 2, 4)
@@ -542,6 +546,14 @@
         ref = weight_piece(level, p, b)
         return remote(ref, piece_send.at[level], piece_recv.at[level, p], dim=target)
 
+    def direct(p, target):
+        ref = weight_piece(1, p, diagonal)
+        return remote(ref, direct_send, direct_recv, dim=target)
+
+    def direct_part():
+        start = line_pieces(fl, PIECES)[RELAYED][0]
+        return weight_part(1, start, fl - start, diagonal)
+
     def tower_rows(member, source):
         return tw.at[member, pl.ds(pl.multiple_of(source * quarter_units, quarter_units), quarter_units), :]
 
@@ -556,7 +568,7 @@
         return (x_next, y_next) if i % 2 == 0 else (y_next, x_next)
 
     def group_of(i):
-        return CROSS + 1 if i == CANDS else i // PIECES
+        return i // PIECES if i < FAR_TOWER else CROSS + i - FAR_TOWER
 
     def plane(i, source, target, arrival):
         return remote(item(i, source), plane_send.at[group_of(i)], arrival, batch=target)
@@ -571,15 +583,22 @@
         plane(i, source, target, plane_recv.at[i]).wait_recv()
         plane(i, source, target, rest_recv.at[group_of(i)]).start()
 
+    def plane_keep(i):
+        source, target = relay(i)
+        plane(i, source, target, plane_recv.at[i]).wait_recv()
+
     def plane_rest(group):
         landed(plane_bytes(group, 2), rest_recv.at[group])
 
     def plane_bytes(group, copies):
+        if group == 1:
+            total = (copies - 1) * fl + line_pieces(fl, PIECES)[RELAYED][0]
+            return flat.at[1, pl.ds(0, total // copies), pl.ds(0, copies * rows_in_part), pl.ds(0, half_k)]
         if group < CROSS:
             return flat.at[group, :, pl.ds(0, copies * rows_in_part), pl.ds(0, half_k)]
-        if group == CROSS + 1:
+        if group == CROSS + 2:
             return cands.at[pl.ds(0, copies)]
-        return tw.at[pl.ds(0, copies * 2), pl.ds(0, quarter_units), :]
+        return tw.at[pl.ds(0, copies), pl.ds(0, quarter_units), :]
 
     def near_tower(target):
         return remote(
@@ -612,7 +631,7 @@
         return remote(rows, unit_send, unit_recv, field=ff, dim=z)
 
     def two(c, ff):
-        lane = pl.multiple_of((1 - ff) * lanes, lanes)
+        lane = pl.multiple_of((1 - part_of) * lanes, lanes)
         return remote(
             y.at[c, :, :, pl.ds(lane, lanes)], two_send, two_recv.at[c],
             to=x2.at[c, pl.ds(ff * fl, fl)], field=other)
@@ -629,16 +648,17 @@
             to=out.at[:, :, rows_of(c)], dim=end)
 
     def part(c):
-        return remote(pre_out.at[c], part_send, part_recv.at[c], to=pre_in.at[c], dim=far)
+        return remote(
+            pre_out.at[c], part_send, part_recv.at[c], to=pre_in.at[c], field=other, dim=far)
 
     def loss_copy(k, c):
         m = lax.rem(me + k, members)
         return remote(
-            losses.at[c], loss_send.at[k], loss_recv, to=loss_out.at[c * field_count + f],
+            losses.at[c], loss_send.at[k], loss_recv, to=loss_out.at[c * field_count + part_of],
             field=m // dim_count, dim=lax.rem(m, dim_count))
 
     def keep_loss(c):
-        return pltpu.make_async_copy(losses.at[c], loss_out.at[c * field_count + f], loss_send.at[0])
+        return pltpu.make_async_copy(losses.at[c], loss_out.at[c * field_count + part_of], loss_send.at[0])
 
     def own_weight(level, ff):
         return pltpu.make_async_copy(
@@ -654,6 +674,17 @@
             weight.at[level, :, ff, pl.ds(row, rows_in_part), :],
             flat.at[level, :, pl.ds(to, rows_in_part), pl.ds(pl.multiple_of(ff * width, width), width)],
             weight_sem.at[level])
+
+    def direct_weight(k):
+        start = line_pieces(fl, PIECES)[RELAYED][0]
+        row = pl.multiple_of(lax.rem(diagonal, 2) * rows_in_part, rows_in_part)
+        ff = diagonal // 2 * (fields // 2) + k
+        to = pl.multiple_of(lax.rem(end, 2) * el + row, rows_in_part)
+        return pltpu.make_async_copy(
+            weight.at[1, pl.ds(start, fl - start), ff, pl.ds(row, rows_in_part), :],
+            flat.at[1, pl.ds(start, fl - start), pl.ds(to, rows_in_part),
+                    pl.ds(pl.multiple_of(ff * width, width), width)],
+            direct_load)
 
     def each(count, act):
         def step(k, carry):
@@ -713,6 +744,7 @@
     @pl.when(is_end)
     def _():
         each(fields // 2, lambda k: end_weight(1, k).start())
+        each(fields // 2, lambda k: direct_weight(k).start())
 
     pl.semaphore_wait(barrier, jnp.where(is_mid, 2 * field_count + 5, 1))
 
@@ -745,22 +777,25 @@
         loaded_end(0)
         for p in range(PIECES - 1):
             piece(0, p, mid).start()
-        for copy in small:
-            copy.wait()
-        pack_tower()
-        pass_in(mid).start()
         for copy in own_features:
             copy.wait()
         from_end(0, mid).start()
         piece(0, PIECES - 1, mid).start()
         from_end(1, mid).start()
+        for copy in small:
+            copy.wait()
         bias_copy(mid).start()
         unit_in(mid).start()
         for c in range(2, chunks):
             from_end(c, mid).start()
+        pack_tower()
+        pass_in(mid).start()
         loaded_end(1)
         for p in range(PIECES):
             piece(1, p, mid).start()
+        pltpu.make_async_copy(direct_part(), direct_part(), direct_load).wait()
+        for p in range(RELAYED, PIECES):
+            direct(p, mid).start()
         near_tower(mid).start()
 
     def expect_piece(level, p):
@@ -811,11 +846,15 @@
             unit_cols[m * units:(m + 1) * units, :] = jnp.broadcast_to(unit_raw[m], (lanes, units)).T
 
     def first(c, carry):
+        @pl.when(c == 1)
+        def _():
+            pass_in(end).wait_recv()
+            pass_on().start()
+
         @pl.when(c == 2)
         def _():
             expect_far(1, 2, far_end)
             plane_forward(FAR_TOWER)
-            plane_forward(END_TOWER)
             expect_piece(1, 0)
 
         @pl.when(c == 3)
@@ -847,10 +886,10 @@
         two(c, f).start()
         give(c).start()
         keep(c).start()
-        for ff in range(field_count):
-            @pl.when(f == ff)
-            def _():
-                x2[c, fs] = y[c, :, :, ff * lanes:(ff + 1) * lanes]
+        for k in range(2):
+            @pl.when(part_of == k)
+            def _():
+                x2[c, fs] = y[c, :, :, k * lanes:(k + 1) * lanes]
 
     def layer_three(c):
         two(c, other).wait_recv()
@@ -870,7 +909,10 @@
 
         @pl.when(c == 1)
         def _():
+            near_tower(end).wait_recv()
+            both(end, f).start()
             expect_one(2)
+            landed(tw.at[pl.ds(0, dim_count)], both_recv)
 
         def tower_step(k, carry):
             layer_three(k)
@@ -894,13 +936,13 @@
         query = lax.dot_general(
             hidden, tw[:, :, side_k:].reshape(members * units, width), (((0,), (0,)), ((), ())),
             preferred_element_type=jnp.float32)
-        start = pl.multiple_of(c * rc + f * lanes, lanes)
+        start = pl.multiple_of(c * rc + part_of * lanes, lanes)
         query_vec = (query + users[pl.ds(start, lanes), :].astype(jnp.float32)).astype(jnp.bfloat16)
         logits = lax.dot_general(
             cands[...].reshape(-1, width), query_vec, (((1,), (1,)), ((), ())),
             preferred_element_type=jnp.float32) * (1.0 / math.sqrt(width))
         labels = lax.broadcasted_iota(jnp.int32, logits.shape, 0)
-        target = targets[c * field_count + f]
+        target = targets[c * field_count + part_of]
         picked = jnp.sum(jnp.where(labels == target, logits, 0.0), axis=0, keepdims=True)
         best = jnp.max(logits, axis=0, keepdims=True)
         total = jnp.sum(jnp.exp(logits - best), axis=0, keepdims=True)
@@ -928,8 +970,6 @@
         expect_far(0, 1, far)
         plane_forward(CANDS)
         expect_piece(0, 2)
-        pass_in(end).wait_recv()
-        pass_on().start()
         expect_far(0, 2, far)
         plane_forward(0)
         plane_forward(1)
@@ -941,7 +981,6 @@
         plane_forward(3)
         expect_far(1, 0, far_end)
         expect_tower(FAR_TOWER, far)
-        expect_tower(END_TOWER, far_end)
         bias_copy(end).wait_recv()
         build_bias()
         unit_in(end).wait_recv()
@@ -955,24 +994,25 @@
         expect_far(1, 1, far_end)
         expect_end(3)
         lax.fori_loop(0, chunks, first, 0)
-        plane_rest(3)
+        plane_rest(4)
         plane_rest(2)
         both(far, f).start()
-        both(far_end, f).start()
         expect_piece(1, 2)
         expect_piece(1, 3)
-        plane_forward(PIECES)
-        plane_forward(PIECES + 1)
+        expect_tower(END_TOWER, far_end)
+        for p in range(RELAYED):
+            plane_forward(PIECES + p)
         expect_one(0)
-        plane_forward(PIECES + 2)
-        plane_forward(PIECES + 3)
+        plane_forward(END_TOWER)
+        for p in range(RELAYED, PIECES):
+            plane_keep(PIECES + p)
         expect_one(1)
-        near_tower(end).wait_recv()
-        both(end, f).start()
         landed(unit_raw.at[pl.ds(0, 6)], unit_recv)
         build_units()
+        plane_rest(3)
+        both(far_end, f).start()
+        landed(direct_part(), direct_recv)
         plane_rest(1)
-        landed(tw.at[pl.ds(0, dim_count)], both_recv)
         lax.fori_loop(0, chunks, second, 0)
 
         @pl.when(owner)
@@ -992,6 +1032,7 @@
     def _():
         for level in range(CROSS):
             sent(weight_part(level, 0, fl, b), piece_send.at[level])
+        sent(direct_part(), direct_send)
         sent(x0.at[:, fs, entries(d), :], end_send)
         bias_copy(mid).wait_send()
         near_tower(mid).wait_send()
@@ -1013,7 +1054,7 @@
         sent(y.at[:, :, :, pl.ds(0, lanes)], two_send)
         sent(out, give_send)
         pltpu.make_async_copy(out, out, out_sem).wait()
-        for group in range(CROSS + 2):
+        for group in range(CROSS + 3):
             sent(plane_bytes(group, 3), plane_send.at[group])
 
     @pl.when(giver)
@@ -1080,7 +1121,7 @@
             dma((CHUNKS,)), dma((CROSS,)), dma((7,)),
             dma, dma((CHUNKS,)), dma((3,)), dma((3, CHUNKS)),
             dma, dma((CHUNKS,)), dma, dma((CHUNKS,)),
-            dma((CROSS,)), dma((CROSS, PIECES)), dma((CROSS + 2,)), dma((items,)), dma((CROSS + 2,)),
+            dma((CROSS,)), dma((CROSS, PIECES)), dma, dma, dma, dma((CROSS + 3,)), dma((items,)), dma((CROSS + 3,)),
             dma((2,)), dma((dim_count,)), dma, dma, dma,
             dma, dma, dma, dma, dma,
             dma, dma((CHUNKS,)), dma, dma, dma, dma, dma((CHUNKS,)), dma((members,)), dma,

time: 103 us -> 102 us (level)
  no operation moved by 1% of the time
where the time goes in v6:
time: 102 us
  Pallas kernels  99.9 us (98%)
  local copies, waits for them, and re-layouts  1.5 us (1%)
    pallas_call x1, Pallas kernels, line_body(): pl.pallas_call(functools.partial(line_kernel, counts), out_shape=(jax.Sha...  99.9 us

profile of v6, /device:TPU:0, one launch (start us, length us, event | category | flops | bytes accessed | tf_op | source)
XLA Modules:
  0.0 102.0 jit_solution(3130330129616782678)
XLA Ops:
  0.6 99.9 %line_forward.1 = (bf16[13,32,1024]{2,1,0:T(8,128)(2,1)S(1)}, f32[8,1,128]{2,1,0:T(1,128)S(1)}) custom-call(bf16[13,32,1024]{2,1,0:T(8,128)(2,1)} %feat.1, bf16[2,13,26,32,128]{4,3,2,1,0:T(8,128)(2,1)} %bitcast.7, f32[13,2,32]{2,1,0:T(2,128)} %bitcast.9, bf16[26,128,128]{2,1,0:T(8,128)(2,1)} %bitcast.8, f32[1,128]{1,0:T(1,128)} %bitcast.11, ...), custom_call_target="tpu_custom_call" | custom-call | tf_op jit(solution)/shard_map/line_forward/pallas_call | solution.py:1090
  100.5 0.9 copy.13
  101.4 0.6 copy.14

commit v7 on v6

--- a/solution.py
+++ b/solution.py
@@ -457,7 +457,7 @@
     feat, weight, bias, tower, tower_bias, query_weight, user, cand, positive,
     out, loss_out,
     x0, x1, y, x2, flat, tw, tw_near, tw_far, tw_pass, tw_raw, q_raw, pre_out, pre_in, pre_own,
-    bias_raw, bias_cols, unit_raw, unit_cols, cands, users, targets, losses,
+    bias_raw, bias_cols, unit_raw, unit_cols, query_cols, cands, users, user_cols, targets, losses,
     feat_sem, weight_sem, small_sem,
     end_send, end_recv, cross_send, cross_recv, pair_send, pair_recv, one_send, one_recv,
     piece_send, piece_recv, direct_load, direct_send, direct_recv, plane_send, plane_recv, rest_recv,
@@ -845,6 +845,16 @@
         for m in range(members):
             unit_cols[m * units:(m + 1) * units, :] = jnp.broadcast_to(unit_raw[m], (lanes, units)).T
 
+    def build_users():
+        for c in range(chunks):
+            start = pl.multiple_of(c * rc + part_of * lanes, lanes)
+            user_cols[c] = users[pl.ds(start, lanes), :].astype(jnp.float32).T
+
+    def build_queries():
+        for m in range(members):
+            block = tw[m, :, side_k:].astype(jnp.float32).T
+            query_cols[:, m * units:(m + 1) * units] = block.astype(jnp.bfloat16)
+
     def first(c, carry):
         @pl.when(c == 1)
         def _():
@@ -897,7 +907,7 @@
 
         @pl.when(owner)
         def _():
-            pre_own[c] = pre
+            pre_own[c] = pre + unit_cols[...]
 
         @pl.when(giver)
         def _():
@@ -931,15 +941,12 @@
 
     def finish(c):
         part(c).wait_recv()
-        pre = pre_own[c] + pre_in[c].astype(jnp.float32) + unit_cols[...]
+        pre = pre_own[c] + pre_in[c].astype(jnp.float32)
         hidden = jnp.maximum(pre, 0.0).astype(jnp.bfloat16)
-        query = lax.dot_general(
-            hidden, tw[:, :, side_k:].reshape(members * units, width), (((0,), (0,)), ((), ())),
-            preferred_element_type=jnp.float32)
-        start = pl.multiple_of(c * rc + part_of * lanes, lanes)
-        query_vec = (query + users[pl.ds(start, lanes), :].astype(jnp.float32)).astype(jnp.bfloat16)
-        logits = lax.dot_general(
-            cands[...].reshape(-1, width), query_vec, (((1,), (1,)), ((), ())),
+        query = jnp.dot(query_cols[...], hidden, preferred_element_type=jnp.float32)
+        query_vec = (query + user_cols[c]).astype(jnp.bfloat16)
+        logits = jnp.dot(
+            cands[...].reshape(-1, width), query_vec,
             preferred_element_type=jnp.float32) * (1.0 / math.sqrt(width))
         labels = lax.broadcasted_iota(jnp.int32, logits.shape, 0)
         target = targets[c * field_count + part_of]
@@ -1009,6 +1016,7 @@
         expect_one(1)
         landed(unit_raw.at[pl.ds(0, 6)], unit_recv)
         build_units()
+        build_users()
         plane_rest(3)
         both(far_end, f).start()
         landed(direct_part(), direct_recv)
@@ -1017,6 +1025,7 @@
 
         @pl.when(owner)
         def _():
+            build_queries()
             for c in range(chunks):
                 finish(c)
 
@@ -1066,6 +1075,17 @@
         for k in range(1, members):
             sent(losses, loss_send.at[k])
         pltpu.make_async_copy(losses, losses, loss_send.at[0]).wait()
+
+
+def emit_kernel(crossed, losses, crossed_out, losses_out, sems):
+    copies = [
+        pltpu.make_async_copy(crossed, crossed_out, sems.at[0]),
+        pltpu.make_async_copy(losses, losses_out, sems.at[1]),
+    ]
+    for copy in copies:
+        copy.start()
+    for copy in copies:
+        copy.wait()
 
 
 def line_body(
@@ -1114,8 +1134,10 @@
             vmem((CROSS, fl * wide, width), f32),
             vmem((members, 1, units), f32),
             vmem((members * units, lanes), f32),
+            vmem((width, members * units), bf16),
             vmem((batch_count,) + candidates.shape, bf16),
             vmem(user_vec.shape, bf16),
+            vmem((CHUNKS, width, lanes), f32),
             vmem((CHUNKS * field_count, 1, lanes), jnp.int32),
             vmem((CHUNKS, 1, lanes), f32),
             dma((CHUNKS,)), dma((CROSS,)), dma((7,)),
@@ -1140,6 +1162,18 @@
         candidates,
         positive.reshape(CHUNKS * field_count, 1, lanes),
     )))
+    crossed, losses = pl.pallas_call(
+        emit_kernel,
+        out_shape=(
+            jax.ShapeDtypeStruct(features.shape, bf16),
+            jax.ShapeDtypeStruct((CHUNKS * field_count, 1, lanes), f32),
+        ),
+        in_specs=[far] * 2,
+        out_specs=(pl.BlockSpec(memory_space=pltpu.HBM),) * 2,
+        scratch_shapes=[dma((2,))],
+        compiler_params=pltpu.CompilerParams(vmem_limit_bytes=4 * 2**20),
+        name="emit",
+    )(crossed, losses)
     return (crossed, losses.reshape(row_count))
 
 

time: 102 us -> 102 us (level)
  local copies, waits for them, and re-layouts: 1.5 us -> 0 us
  Pallas kernels: 99.9 us -> 101 us
    unnamed x2 -> x0, local copies, waits for them, and re-layouts: 1.5 us -> none
where the time goes in v7:
time: 102 us; the launch traced here: 101 us
  Pallas kernels  101 us (99%)
    pallas_call x1, Pallas kernels, line_body(): pl.pallas_call(functools.partial(line_kernel, counts), out_shape=(jax.Sha...  99.9 us

profile of v7, /device:TPU:0, one launch (start us, length us, event | category | flops | bytes accessed | tf_op | source)
XLA Modules:
  0.0 101.4 jit_solution(7702008683047666734)
XLA Ops:
  0.6 99.9 %line_forward.1 = (bf16[13,32,1024]{2,1,0:T(8,128)(2,1)S(1)}, f32[8,1,128]{2,1,0:T(1,128)S(1)}) custom-call(bf16[13,32,1024]{2,1,0:T(8,128)(2,1)} %feat.1, bf16[2,13,26,32,128]{4,3,2,1,0:T(8,128)(2,1)} %bitcast.6, f32[13,2,32]{2,1,0:T(2,128)} %bitcast.8, bf16[26,128,128]{2,1,0:T(8,128)(2,1)} %bitcast.7, f32[1,128]{1,0:T(1,128)} %bitcast.10, ...), custom_call_target="tpu_custom_call" | custom-call | tf_op jit(solution)/shard_map/line_forward/pallas_call | solution.py:1110
  100.5 0.9 emit.1

commit v8 on v7

--- a/solution.py
+++ b/solution.py
@@ -652,10 +652,12 @@
             pre_out.at[c], part_send, part_recv.at[c], to=pre_in.at[c], field=other, dim=far)
 
     def loss_copy(k, c):
-        m = lax.rem(me + k, members)
+        ff, z = (
+            (other, far_end), (f, far_end), (other, end), (other, far), (f, end), (f, far), (other, d),
+        )[k - 1]
         return remote(
             losses.at[c], loss_send.at[k], loss_recv, to=loss_out.at[c * field_count + part_of],
-            field=m // dim_count, dim=lax.rem(m, dim_count))
+            field=ff, dim=z)
 
     def keep_loss(c):
         return pltpu.make_async_copy(losses.at[c], loss_out.at[c * field_count + part_of], loss_send.at[0])

time: 102 us -> 102 us (level)
  no operation moved by 1% of the time
where the time goes in v8:
time: 102 us; the launch traced here: 101 us
  Pallas kernels  101 us (99%)
    pallas_call x1, Pallas kernels, line_body(): pl.pallas_call(functools.partial(line_kernel, counts), out_shape=(jax.Sha...  99.9 us

profile of v8, /device:TPU:0, one launch (start us, length us, event | category | flops | bytes accessed | tf_op | source)
XLA Modules:
  0.0 101.4 jit_solution(16134270904492738152)
XLA Ops:
  0.6 99.9 %line_forward.1 = (bf16[13,32,1024]{2,1,0:T(8,128)(2,1)S(1)}, f32[8,1,128]{2,1,0:T(1,128)S(1)}) custom-call(bf16[13,32,1024]{2,1,0:T(8,128)(2,1)} %feat.1, bf16[2,13,26,32,128]{4,3,2,1,0:T(8,128)(2,1)} %bitcast.6, f32[13,2,32]{2,1,0:T(2,128)} %bitcast.8, bf16[26,128,128]{2,1,0:T(8,128)(2,1)} %bitcast.7, f32[1,128]{1,0:T(1,128)} %bitcast.10, ...), custom_call_target="tpu_custom_call" | custom-call | tf_op jit(solution)/shard_map/line_forward/pallas_call | solution.py:1112
  100.5 0.9 emit.1

commit v9 on v8

--- a/solution.py
+++ b/solution.py
@@ -647,9 +647,11 @@
             y.at[c, :, within(end), :], give_send, give_recv,
             to=out.at[:, :, rows_of(c)], dim=end)
 
-    def part(c):
+    def part(last):
+        rows = pl.ds(chunks - 1, 1) if last else pl.ds(0, chunks - 1)
         return remote(
-            pre_out.at[c], part_send, part_recv.at[c], to=pre_in.at[c], field=other, dim=far)
+            pre_out.at[rows], part_send, part_recv.at[last], to=pre_in.at[rows],
+            field=other, dim=far)
 
     def loss_copy(k, c):
         ff, z = (
@@ -914,7 +916,15 @@
         @pl.when(giver)
         def _():
             pre_out[c] = pre.astype(jnp.bfloat16)
-            part(c).start()
+
+    def give_parts(c):
+        @pl.when(giver & (c == chunks - 2))
+        def _():
+            part(0).start()
+
+        @pl.when(giver & (c == chunks - 1))
+        def _():
+            part(1).start()
 
     def second(c, carry):
         layer_two(c)
@@ -928,6 +938,7 @@
 
         def tower_step(k, carry):
             layer_three(k)
+            give_parts(k)
             return carry
 
         last = c == chunks - 1
@@ -942,7 +953,10 @@
         return carry
 
     def finish(c):
-        part(c).wait_recv()
+        if c == 0:
+            part(0).wait_recv()
+        if c == chunks - 1:
+            part(1).wait_recv()
         pre = pre_own[c] + pre_in[c].astype(jnp.float32)
         hidden = jnp.maximum(pre, 0.0).astype(jnp.bfloat16)
         query = jnp.dot(query_cols[...], hidden, preferred_element_type=jnp.float32)
@@ -1148,7 +1162,7 @@
             dma((CROSS,)), dma((CROSS, PIECES)), dma, dma, dma, dma((CROSS + 3,)), dma((items,)), dma((CROSS + 3,)),
             dma((2,)), dma((dim_count,)), dma, dma, dma,
             dma, dma, dma, dma, dma,
-            dma, dma((CHUNKS,)), dma, dma, dma, dma, dma((CHUNKS,)), dma((members,)), dma,
+            dma, dma((CHUNKS,)), dma, dma, dma, dma, dma((2,)), dma((members,)), dma,
         ],
         compiler_params=pltpu.CompilerParams(
             collective_id=0, has_side_effects=True, vmem_limit_bytes=48 * 2**20),

time: 102 us -> 103 us (level)
    pallas_call x1, Pallas kernels: 99.9 us -> 101 us  [line_body(): pl.pallas_call(functools.partial(line_kernel, counts), out_shape=(jax.Sha...]
where the time goes in v9:
time: 103 us
  Pallas kernels  102 us (99%)
    pallas_call x1, Pallas kernels, line_body(): pl.pallas_call(functools.partial(line_kernel, counts), out_shape=(jax.Sha...  101 us

profile of v9, /device:TPU:0, one launch (start us, length us, event | category | flops | bytes accessed | tf_op | source)
XLA Modules:
  0.0 102.5 jit_solution(13415231809087833610)
XLA Ops:
  0.6 101.0 %line_forward.1 = (bf16[13,32,1024]{2,1,0:T(8,128)(2,1)S(1)}, f32[8,1,128]{2,1,0:T(1,128)S(1)}) custom-call(bf16[13,32,1024]{2,1,0:T(8,128)(2,1)} %feat.1, bf16[2,13,26,32,128]{4,3,2,1,0:T(8,128)(2,1)} %bitcast.6, f32[13,2,32]{2,1,0:T(2,128)} %bitcast.8, bf16[26,128,128]{2,1,0:T(8,128)(2,1)} %bitcast.7, f32[1,128]{1,0:T(1,128)} %bitcast.10, ...), custom_call_target="tpu_custom_call" | custom-call | tf_op jit(solution)/shard_map/line_forward/pallas_call | solution.py:1126
  101.6 0.9 emit.1
